TPU v7x, 256 devices: a whole 4x4x8 slice. The times are simulated.
256 devices in a mesh: outer: 8 (over z_hi, core), inner: 8 (over x, z_lo), head: 4 (over y).
Axes of the slice: x: 4, y: 4, z: 8 (z_hi: 4, z_lo: 2; z = z_hi * 2 + z_lo), core: 2. Of those that a mesh axis runs over, the one named last changes fastest.
Arguments:
- stored_query_rows: bfloat16 [16384, 32, 128], P(('outer', 'inner'), 'head'), may hold values from -12 to 12
- stored_key_rows: bfloat16 [16384, 8, 128], P(('outer', 'inner'), 'head'), may hold values from -12 to 12
- stored_value_rows: bfloat16 [16384, 8, 128], P(('outer', 'inner'), 'head'), may hold values from -6 to 6
- span_order: int32 [128], replicated, may hold values from 0 to 127, each once
Outputs:
- attended: bfloat16 [16384, 32, 128], P(('outer', 'inner'), 'head')
Inputs may be any that keep to these rules, and one draw needn't show every extreme that they name: `span_order`: a permutation of the sequence's 128 blocks of 128 tokens.
All inputs are finite; a program needn't handle non-finite values.
Results may differ from a plain program's by a relative error of at most 0.0075.
Values may be sent and summed in bfloat16 or wider, within the bound.
A program may use at most 128 MiB of HBM per device.

v0:
```python
import math

import jax
import jax.numpy as jnp
from jax import lax
from jax.sharding import PartitionSpec as P


def in_one_piece(arrays, axis, dim, along):
    ends, at = ([], 0)
    for a in arrays[:-1]:
        at += a.shape[along]
        ends.append(at)
    both = jnp.concatenate(arrays, axis=along)
    return tuple(jnp.split(lax.all_gather(both, axis, axis=dim, tiled=True), ends, axis=along))


def sent_to_all(x, axis):
    copies = jnp.broadcast_to(x, (lax.axis_size(axis), *x.shape))
    return lax.all_to_all(copies, axis, split_axis=0, concat_axis=0, tiled=True)


def over_copies(x, axis):
    everything = sent_to_all(x, axis)
    return jnp.max(everything, axis=0)


def sent_together(arrays, axis, dim, along):
    widths = [math.prod(a.shape[along:]) for a in arrays]
    both = jnp.concatenate(
        [a.reshape(*a.shape[:along], w) for a, w in zip(arrays, widths)], axis=along
    )
    whole = lax.psum_scatter(both, axis, scatter_dimension=dim, tiled=True)
    pieces = jnp.split(whole, [sum(widths[:k]) for k in range(1, len(widths))], axis=along)
    return tuple(
        (b.reshape(*whole.shape[:along], *a.shape[along:]) for a, b in zip(arrays, pieces))
    )


def attend_block(carry, query_tile, key_tile, value_tile, allowed, score_scale):
    run_max, run_sum, run_acc = carry
    scores = (
        jnp.einsum("ghqa,kga->ghqk", query_tile, key_tile, preferred_element_type=jnp.float32)
        * score_scale
    )
    scores = jnp.where(allowed[None, None], scores, -1e30)
    new_max = jnp.maximum(run_max, jnp.max(scores, axis=-1))
    weights = jnp.where(allowed[None, None], jnp.exp(scores - new_max[..., None]), 0.0)
    rescale = jnp.exp(run_max - new_max)
    new_sum = run_sum * rescale + jnp.sum(weights, axis=-1)
    added = jnp.einsum(
        "ghqk,kga->ghqa",
        weights.astype(jnp.bfloat16),
        value_tile,
        preferred_element_type=jnp.float32,
    )
    return (new_max, new_sum, run_acc * rescale[..., None] + added)


def block_peak(current, query_tile, key_tile, allowed, score_scale):
    scores = (
        jnp.einsum("ghqa,kga->ghqk", query_tile, key_tile, preferred_element_type=jnp.float32)
        * score_scale
    )
    scores = jnp.where(allowed[None, None], scores, -1e30)
    return jnp.maximum(current, jnp.max(scores, axis=-1))


def body(stored_query_rows, stored_key_rows, stored_value_rows, span_order):
    row_count = stored_query_rows.shape[0]
    span_rows = row_count // 2
    kv_groups = stored_key_rows.shape[1]
    per_group = stored_query_rows.shape[1] // kv_groups
    head_width = stored_query_rows.shape[2]
    score_scale = 1.0 / math.sqrt(head_width)
    outer_count = lax.axis_size("outer")
    inner_count = lax.axis_size("inner")
    outer_here = lax.axis_index("outer")
    inner_here = lax.axis_index("inner")
    offsets = jnp.arange(span_rows, dtype=jnp.int32)
    kv_near = in_one_piece((stored_key_rows, stored_value_rows), "inner", 0, 1)
    query_far = lax.all_gather(stored_query_rows, "outer", axis=0, tiled=True)
    query_blocks = 2 * outer_count
    key_blocks = 2 * inner_count
    query_stack = query_far.reshape(
        query_blocks, span_rows, kv_groups, per_group, head_width
    ).transpose(0, 2, 3, 1, 4)
    block_numbers = jnp.arange(query_blocks, dtype=jnp.int32)

    def query_anchor_of(block_q):
        return span_order[(block_q // 2 * inner_count + inner_here) * 2 + block_q % 2]

    def key_anchor_of(block_k):
        return span_order[(outer_here * inner_count + block_k // 2) * 2 + block_k % 2]

    def local_peak(packed):
        query_tile, block_q = packed
        query_anchor = query_anchor_of(block_q)
        query_pos = query_anchor * span_rows + offsets

        def local_visit_key(block_k, current):
            key_tile = lax.dynamic_slice_in_dim(kv_near[0], block_k * span_rows, span_rows, 0)
            key_anchor = key_anchor_of(block_k)
            allowed = (key_anchor * span_rows + offsets)[None, :] <= query_pos[:, None]
            return lax.cond(
                key_anchor <= query_anchor,
                lambda held: block_peak(held, query_tile, key_tile, allowed, score_scale),
                lambda held: held,
                current,
            )

        start_peak = jnp.full((kv_groups, per_group, span_rows), -1e30, jnp.float32)
        return lax.fori_loop(0, key_blocks, local_visit_key, start_peak)

    maxima = lax.map(local_peak, (query_stack, block_numbers))
    peak = over_copies(maxima, "outer")

    def one_query(packed):
        query_tile, block_q, row_peak = packed
        query_anchor = query_anchor_of(block_q)
        query_pos = query_anchor * span_rows + offsets

        def one_visit_key(block_k, state):
            key_tile = lax.dynamic_slice_in_dim(kv_near[0], block_k * span_rows, span_rows, 0)
            value_tile = lax.dynamic_slice_in_dim(kv_near[1], block_k * span_rows, span_rows, 0)
            key_anchor = key_anchor_of(block_k)
            allowed = (key_anchor * span_rows + offsets)[None, :] <= query_pos[:, None]
            return lax.cond(
                key_anchor <= query_anchor,
                lambda carried: attend_block(
                    carried, query_tile, key_tile, value_tile, allowed, score_scale
                ),
                lambda carried: carried,
                state,
            )

        begin = (
            row_peak,
            jnp.zeros((kv_groups, per_group, span_rows), jnp.float32),
            jnp.zeros((kv_groups, per_group, span_rows, head_width), jnp.float32),
        )
        final = lax.fori_loop(0, key_blocks, one_visit_key, begin)
        return (final[1], final[2])

    totals, sums = lax.map(one_query, (query_stack, block_numbers, peak))
    shares = sent_together((sums, totals), "outer", 0, 4)
    result = shares[0] / shares[1][..., None]
    result = result.transpose(0, 3, 1, 2, 4).reshape(row_count, kv_groups * per_group, head_width)
    return result.astype(jnp.bfloat16)


def solution(mesh):
    placed = (
        P(("outer", "inner"), "head", None),
        P(("outer", "inner"), "head", None),
        P(("outer", "inner"), "head", None),
        P(),
    )
    return jax.shard_map(
        body,
        mesh=mesh,
        in_specs=placed,
        out_specs=P(("outer", "inner"), "head", None),
        check_vma=False,
    )
```

profile of v0, /device:TPU:1, one launch (start us, length us, event | category | flops | bytes accessed | tf_op | source)
XLA Modules:
  0.0 1938.8 jit_solution(18340731163666808901)
XLA Ops:
  9.2 1.9 copy.19
  11.2 55.9 %all-gather.5.cloned.1.call-done = bf16[2048,4,128]{2,0,1:T(8,128)(2,1)} async-done(((bf16[256,4,128]{2,0,1:T(8,128)(2,1)}), bf16[2048,4,128]{2,0,1:T(8,128)(2,1)}) %all-gather.5.cloned.1.call-update) | async-done | bytes 2097168 | tf_op jit(solution)/shard_map/all_gather | solution.py:15
  67.1 1.7 fusion.28
  68.7 53.5 %all-gather.3.cloned.1.call-done = bf16[2048,8,128]{2,0,1:T(8,128)(2,1)} async-done(((bf16[256,8,128]{2,0,1:T(8,128)(2,1)}), bf16[2048,8,128]{2,0,1:T(8,128)(2,1)}) %all-gather.3.cloned.1.call-update) | async-done | bytes 4194320 | tf_op jit(solution)/shard_map/all_gather | solution.py:82
  122.2 4.7 copy.22
  126.9 698.5 %while.103 = (s32[]{:T(128)}, f32[16,2,4,128]{3,0,2,1:T(8,128)S(1)}, s32[16]{0:T(128)S(1)}, s32[]{:T(128)}, s32[128]{0:T(128)S(1)}, /*index=5*/bf16[16,2,4,128,1...) while((s32[]{:T(128)}, f32[16,2,4,128]{3,0,2,1:T(8,128)S(1)}, ...), condition=%wide.region_6.7_spmd.clone.clone, body=%wide.region_0.6_spmd.clone.clone.sunk | while | flops 33964340 | bytes 917600 | solution.py:115
  132.3 37.2 %while.106 = (s32[]{:T(128)}, f32[2,4,128]{2,1,0:T(4,128)S(1)}, s32[]{:T(128)}, s32[128]{0:T(128)S(1)}, s32[]{:T(128)}, /*index=5*/s32[128]{0:T(128)S(1)}, s32[1...) while((s32[]{:T(128)}, f32[2,4,128]{2,1,0:T(4,128)S(1)}, ...), condition=%wide.region_5.5_spmd, body=%wide.region_1.4_spmd.sunk | while | flops 33964184 | bytes 379362 | solution.py:113
  174.8 37.2 %while.106 = (s32[]{:T(128)}, f32[2,4,128]{2,1,0:T(4,128)S(1)}, s32[]{:T(128)}, s32[128]{0:T(128)S(1)}, s32[]{:T(128)}, /*index=5*/s32[128]{0:T(128)S(1)}, s32[1...) while((s32[]{:T(128)}, f32[2,4,128]{2,1,0:T(4,128)S(1)}, ...), condition=%wide.region_5.5_spmd, body=%wide.region_1.4_spmd.sunk | while | flops 33964184 | bytes 379362 | solution.py:113
  217.4 46.2 %while.106 = (s32[]{:T(128)}, f32[2,4,128]{2,1,0:T(4,128)S(1)}, s32[]{:T(128)}, s32[128]{0:T(128)S(1)}, s32[]{:T(128)}, /*index=5*/s32[128]{0:T(128)S(1)}, s32[1...) while((s32[]{:T(128)}, f32[2,4,128]{2,1,0:T(4,128)S(1)}, ...), condition=%wide.region_5.5_spmd, body=%wide.region_1.4_spmd.sunk | while | flops 33964184 | bytes 379362 | solution.py:113
  269.0 42.2 %while.106 = (s32[]{:T(128)}, f32[2,4,128]{2,1,0:T(4,128)S(1)}, s32[]{:T(128)}, s32[128]{0:T(128)S(1)}, s32[]{:T(128)}, /*index=5*/s32[128]{0:T(128)S(1)}, s32[1...) while((s32[]{:T(128)}, f32[2,4,128]{2,1,0:T(4,128)S(1)}, ...), condition=%wide.region_5.5_spmd, body=%wide.region_1.4_spmd.sunk | while | flops 33964184 | bytes 379362 | solution.py:113
  316.6 37.2 %while.106 = (s32[]{:T(128)}, f32[2,4,128]{2,1,0:T(4,128)S(1)}, s32[]{:T(128)}, s32[128]{0:T(128)S(1)}, s32[]{:T(128)}, /*index=5*/s32[128]{0:T(128)S(1)}, s32[1...) while((s32[]{:T(128)}, f32[2,4,128]{2,1,0:T(4,128)S(1)}, ...), condition=%wide.region_5.5_spmd, body=%wide.region_1.4_spmd.sunk | while | flops 33964184 | bytes 379362 | solution.py:113
  359.2 45.2 %while.106 = (s32[]{:T(128)}, f32[2,4,128]{2,1,0:T(4,128)S(1)}, s32[]{:T(128)}, s32[128]{0:T(128)S(1)}, s32[]{:T(128)}, /*index=5*/s32[128]{0:T(128)S(1)}, s32[1...) while((s32[]{:T(128)}, f32[2,4,128]{2,1,0:T(4,128)S(1)}, ...), condition=%wide.region_5.5_spmd, body=%wide.region_1.4_spmd.sunk | while | flops 33964184 | bytes 379362 | solution.py:113
  409.8 45.2 %while.106 = (s32[]{:T(128)}, f32[2,4,128]{2,1,0:T(4,128)S(1)}, s32[]{:T(128)}, s32[128]{0:T(128)S(1)}, s32[]{:T(128)}, /*index=5*/s32[128]{0:T(128)S(1)}, s32[1...) while((s32[]{:T(128)}, f32[2,4,128]{2,1,0:T(4,128)S(1)}, ...), condition=%wide.region_5.5_spmd, body=%wide.region_1.4_spmd.sunk | while | flops 33964184 | bytes 379362 | solution.py:113
  460.4 34.2 %while.106 = (s32[]{:T(128)}, f32[2,4,128]{2,1,0:T(4,128)S(1)}, s32[]{:T(128)}, s32[128]{0:T(128)S(1)}, s32[]{:T(128)}, /*index=5*/s32[128]{0:T(128)S(1)}, s32[1...) while((s32[]{:T(128)}, f32[2,4,128]{2,1,0:T(4,128)S(1)}, ...), condition=%wide.region_5.5_spmd, body=%wide.region_1.4_spmd.sunk | while | flops 33964184 | bytes 379362 | solution.py:113
  500.0 35.2 %while.106 = (s32[]{:T(128)}, f32[2,4,128]{2,1,0:T(4,128)S(1)}, s32[]{:T(128)}, s32[128]{0:T(128)S(1)}, s32[]{:T(128)}, /*index=5*/s32[128]{0:T(128)S(1)}, s32[1...) while((s32[]{:T(128)}, f32[2,4,128]{2,1,0:T(4,128)S(1)}, ...), condition=%wide.region_5.5_spmd, body=%wide.region_1.4_spmd.sunk | while | flops 33964184 | bytes 379362 | solution.py:113
  540.6 37.2 %while.106 = (s32[]{:T(128)}, f32[2,4,128]{2,1,0:T(4,128)S(1)}, s32[]{:T(128)}, s32[128]{0:T(128)S(1)}, s32[]{:T(128)}, /*index=5*/s32[128]{0:T(128)S(1)}, s32[1...) while((s32[]{:T(128)}, f32[2,4,128]{2,1,0:T(4,128)S(1)}, ...), condition=%wide.region_5.5_spmd, body=%wide.region_1.4_spmd.sunk | while | flops 33964184 | bytes 379362 | solution.py:113
  583.2 32.2 %while.106 = (s32[]{:T(128)}, f32[2,4,128]{2,1,0:T(4,128)S(1)}, s32[]{:T(128)}, s32[128]{0:T(128)S(1)}, s32[]{:T(128)}, /*index=5*/s32[128]{0:T(128)S(1)}, s32[1...) while((s32[]{:T(128)}, f32[2,4,128]{2,1,0:T(4,128)S(1)}, ...), condition=%wide.region_5.5_spmd, body=%wide.region_1.4_spmd.sunk | while | flops 33964184 | bytes 379362 | solution.py:113
  620.8 37.2 %while.106 = (s32[]{:T(128)}, f32[2,4,128]{2,1,0:T(4,128)S(1)}, s32[]{:T(128)}, s32[128]{0:T(128)S(1)}, s32[]{:T(128)}, /*index=5*/s32[128]{0:T(128)S(1)}, s32[1...) while((s32[]{:T(128)}, f32[2,4,128]{2,1,0:T(4,128)S(1)}, ...), condition=%wide.region_5.5_spmd, body=%wide.region_1.4_spmd.sunk | while | flops 33964184 | bytes 379362 | solution.py:113
  663.4 37.2 %while.106 = (s32[]{:T(128)}, f32[2,4,128]{2,1,0:T(4,128)S(1)}, s32[]{:T(128)}, s32[128]{0:T(128)S(1)}, s32[]{:T(128)}, /*index=5*/s32[128]{0:T(128)S(1)}, s32[1...) while((s32[]{:T(128)}, f32[2,4,128]{2,1,0:T(4,128)S(1)}, ...), condition=%wide.region_5.5_spmd, body=%wide.region_1.4_spmd.sunk | while | flops 33964184 | bytes 379362 | solution.py:113
  706.0 36.2 %while.106 = (s32[]{:T(128)}, f32[2,4,128]{2,1,0:T(4,128)S(1)}, s32[]{:T(128)}, s32[128]{0:T(128)S(1)}, s32[]{:T(128)}, /*index=5*/s32[128]{0:T(128)S(1)}, s32[1...) while((s32[]{:T(128)}, f32[2,4,128]{2,1,0:T(4,128)S(1)}, ...), condition=%wide.region_5.5_spmd, body=%wide.region_1.4_spmd.sunk | while | flops 33964184 | bytes 379362 | solution.py:113
  747.6 35.2 %while.106 = (s32[]{:T(128)}, f32[2,4,128]{2,1,0:T(4,128)S(1)}, s32[]{:T(128)}, s32[128]{0:T(128)S(1)}, s32[]{:T(128)}, /*index=5*/s32[128]{0:T(128)S(1)}, s32[1...) while((s32[]{:T(128)}, f32[2,4,128]{2,1,0:T(4,128)S(1)}, ...), condition=%wide.region_5.5_spmd, body=%wide.region_1.4_spmd.sunk | while | flops 33964184 | bytes 379362 | solution.py:113
  788.2 37.2 %while.106 = (s32[]{:T(128)}, f32[2,4,128]{2,1,0:T(4,128)S(1)}, s32[]{:T(128)}, s32[128]{0:T(128)S(1)}, s32[]{:T(128)}, /*index=5*/s32[128]{0:T(128)S(1)}, s32[1...) while((s32[]{:T(128)}, f32[2,4,128]{2,1,0:T(4,128)S(1)}, ...), condition=%wide.region_5.5_spmd, body=%wide.region_1.4_spmd.sunk | while | flops 33964184 | bytes 379362 | solution.py:113
  826.3 35.9 %all-to-all-start = ((f32[8,16,2,4,128]{4,1,3,2,0:T(8,128)}), f32[8,16,2,4,128]{4,1,3,2,0:T(8,128)S(1)}, u32[]{:S(2)}, u32[]{:S(2)}) async-start(f32[8,16,2,4,128]{4,1,3,2,0:T(8,128)} %broadcast_in_dim.92), calls=%async_computation | async-start | bytes 1048576 | tf_op jit(solution)/shard_map/all_to_all | solution.py:20
  862.2 13.0 all-to-all-done
  875.3 764.1 %while.105 = (s32[]{:T(128)}, f32[16,2,4,128]{3,2,1,0:T(4,128)S(1)}, f32[16,2,4,128,128]{4,3,2,1,0:T(8,128)}, f32[16,2,4,128]{3,0,2,1:T(8,128)S(1)}, s32[16]{0:T...) while((s32[]{:T(128)}, f32[16,2,4,128]{3,2,1,0:T(4,128)S(1)}, ...), condition=%wide.region_15.16_spmd.clone.clone, body=%wide.region_8.15_spmd.clone.clone.sunk | while | flops 68569392 | bytes 5267704 | solution.py:145
  880.7 39.9 %while.107 = (s32[]{:T(128)}, f32[2,4,128]{2,1,0:T(4,128)S(1)}, f32[2,4,128]{2,1,0:T(4,128)S(1)}, f32[2,4,128,128]{3,2,1,0:T(8,128)S(1)}, s32[]{:T(128)}, /*inde...) while((s32[]{:T(128)}, f32[2,4,128]{2,1,0:T(4,128)S(1)}, ...), condition=%wide.region_14.14_spmd, body=%wide.region_9.13_spmd.sunk | while | flops 68569240 | bytes 3148358 | solution.py:142
  893.1 1.6 conditional.4
  926.8 39.9 %while.107 = (s32[]{:T(128)}, f32[2,4,128]{2,1,0:T(4,128)S(1)}, f32[2,4,128]{2,1,0:T(4,128)S(1)}, f32[2,4,128,128]{3,2,1,0:T(8,128)S(1)}, s32[]{:T(128)}, /*inde...) while((s32[]{:T(128)}, f32[2,4,128]{2,1,0:T(4,128)S(1)}, ...), condition=%wide.region_14.14_spmd, body=%wide.region_9.13_spmd.sunk | while | flops 68569240 | bytes 3148358 | solution.py:142
  934.1 1.6 conditional.4
  972.9 53.8 %while.107 = (s32[]{:T(128)}, f32[2,4,128]{2,1,0:T(4,128)S(1)}, f32[2,4,128]{2,1,0:T(4,128)S(1)}, f32[2,4,128,128]{3,2,1,0:T(8,128)S(1)}, s32[]{:T(128)}, /*inde...) while((s32[]{:T(128)}, f32[2,4,128]{2,1,0:T(4,128)S(1)}, ...), condition=%wide.region_14.14_spmd, body=%wide.region_9.13_spmd.sunk | while | flops 68569240 | bytes 3148358 | solution.py:142
  1032.9 47.6 %while.107 = (s32[]{:T(128)}, f32[2,4,128]{2,1,0:T(4,128)S(1)}, f32[2,4,128]{2,1,0:T(4,128)S(1)}, f32[2,4,128,128]{3,2,1,0:T(8,128)S(1)}, s32[]{:T(128)}, /*inde...) while((s32[]{:T(128)}, f32[2,4,128]{2,1,0:T(4,128)S(1)}, ...), condition=%wide.region_14.14_spmd, body=%wide.region_9.13_spmd.sunk | while | flops 68569240 | bytes 3148358 | solution.py:142
  1041.7 1.6 conditional.4
  1052.1 1.6 conditional.4
  1086.8 39.9 %while.107 = (s32[]{:T(128)}, f32[2,4,128]{2,1,0:T(4,128)S(1)}, f32[2,4,128]{2,1,0:T(4,128)S(1)}, f32[2,4,128,128]{3,2,1,0:T(8,128)S(1)}, s32[]{:T(128)}, /*inde...) while((s32[]{:T(128)}, f32[2,4,128]{2,1,0:T(4,128)S(1)}, ...), condition=%wide.region_14.14_spmd, body=%wide.region_9.13_spmd.sunk | while | flops 68569240 | bytes 3148358 | solution.py:142
  1104.4 1.6 conditional.4
  1132.9 52.2 %while.107 = (s32[]{:T(128)}, f32[2,4,128]{2,1,0:T(4,128)S(1)}, f32[2,4,128]{2,1,0:T(4,128)S(1)}, f32[2,4,128,128]{3,2,1,0:T(8,128)S(1)}, s32[]{:T(128)}, /*inde...) while((s32[]{:T(128)}, f32[2,4,128]{2,1,0:T(4,128)S(1)}, ...), condition=%wide.region_14.14_spmd, body=%wide.region_9.13_spmd.sunk | while | flops 68569240 | bytes 3148358 | solution.py:142
  1191.3 52.2 %while.107 = (s32[]{:T(128)}, f32[2,4,128]{2,1,0:T(4,128)S(1)}, f32[2,4,128]{2,1,0:T(4,128)S(1)}, f32[2,4,128,128]{3,2,1,0:T(8,128)S(1)}, s32[]{:T(128)}, /*inde...) while((s32[]{:T(128)}, f32[2,4,128]{2,1,0:T(4,128)S(1)}, ...), condition=%wide.region_14.14_spmd, body=%wide.region_9.13_spmd.sunk | while | flops 68569240 | bytes 3148358 | solution.py:142
  1198.3 1.6 conditional.4
  1249.8 35.2 %while.107 = (s32[]{:T(128)}, f32[2,4,128]{2,1,0:T(4,128)S(1)}, f32[2,4,128]{2,1,0:T(4,128)S(1)}, f32[2,4,128,128]{3,2,1,0:T(8,128)S(1)}, s32[]{:T(128)}, /*inde...) while((s32[]{:T(128)}, f32[2,4,128]{2,1,0:T(4,128)S(1)}, ...), condition=%wide.region_14.14_spmd, body=%wide.region_9.13_spmd.sunk | while | flops 68569240 | bytes 3148358 | solution.py:142
  1291.3 36.8 %while.107 = (s32[]{:T(128)}, f32[2,4,128]{2,1,0:T(4,128)S(1)}, f32[2,4,128]{2,1,0:T(4,128)S(1)}, f32[2,4,128,128]{3,2,1,0:T(8,128)S(1)}, s32[]{:T(128)}, /*inde...) while((s32[]{:T(128)}, f32[2,4,128]{2,1,0:T(4,128)S(1)}, ...), condition=%wide.region_14.14_spmd, body=%wide.region_9.13_spmd.sunk | while | flops 68569240 | bytes 3148358 | solution.py:142
  1326.5 1.6 conditional.4
  1334.3 39.9 %while.107 = (s32[]{:T(128)}, f32[2,4,128]{2,1,0:T(4,128)S(1)}, f32[2,4,128]{2,1,0:T(4,128)S(1)}, f32[2,4,128,128]{3,2,1,0:T(8,128)S(1)}, s32[]{:T(128)}, /*inde...) while((s32[]{:T(128)}, f32[2,4,128]{2,1,0:T(4,128)S(1)}, ...), condition=%wide.region_14.14_spmd, body=%wide.region_9.13_spmd.sunk | while | flops 68569240 | bytes 3148358 | solution.py:142
  1364.0 1.6 conditional.4
  1372.6 1.6 conditional.4
  1380.4 32.1 %while.107 = (s32[]{:T(128)}, f32[2,4,128]{2,1,0:T(4,128)S(1)}, f32[2,4,128]{2,1,0:T(4,128)S(1)}, f32[2,4,128,128]{3,2,1,0:T(8,128)S(1)}, s32[]{:T(128)}, /*inde...) while((s32[]{:T(128)}, f32[2,4,128]{2,1,0:T(4,128)S(1)}, ...), condition=%wide.region_14.14_spmd, body=%wide.region_9.13_spmd.sunk | while | flops 68569240 | bytes 3148358 | solution.py:142
  1418.8 39.9 %while.107 = (s32[]{:T(128)}, f32[2,4,128]{2,1,0:T(4,128)S(1)}, f32[2,4,128]{2,1,0:T(4,128)S(1)}, f32[2,4,128,128]{3,2,1,0:T(8,128)S(1)}, s32[]{:T(128)}, /*inde...) while((s32[]{:T(128)}, f32[2,4,128]{2,1,0:T(4,128)S(1)}, ...), condition=%wide.region_14.14_spmd, body=%wide.region_9.13_spmd.sunk | while | flops 68569240 | bytes 3148358 | solution.py:142
  1431.2 1.6 conditional.4
  1464.9 39.9 %while.107 = (s32[]{:T(128)}, f32[2,4,128]{2,1,0:T(4,128)S(1)}, f32[2,4,128]{2,1,0:T(4,128)S(1)}, f32[2,4,128,128]{3,2,1,0:T(8,128)S(1)}, s32[]{:T(128)}, /*inde...) while((s32[]{:T(128)}, f32[2,4,128]{2,1,0:T(4,128)S(1)}, ...), condition=%wide.region_14.14_spmd, body=%wide.region_9.13_spmd.sunk | while | flops 68569240 | bytes 3148358 | solution.py:142
  1482.5 1.6 conditional.4
  1511.0 38.3 %while.107 = (s32[]{:T(128)}, f32[2,4,128]{2,1,0:T(4,128)S(1)}, f32[2,4,128]{2,1,0:T(4,128)S(1)}, f32[2,4,128,128]{3,2,1,0:T(8,128)S(1)}, s32[]{:T(128)}, /*inde...) while((s32[]{:T(128)}, f32[2,4,128]{2,1,0:T(4,128)S(1)}, ...), condition=%wide.region_14.14_spmd, body=%wide.region_9.13_spmd.sunk | while | flops 68569240 | bytes 3148358 | solution.py:142
  1523.4 1.6 conditional.4
  1539.3 1.6 conditional.4
  1547.8 1.6 conditional.4
  1555.6 36.8 %while.107 = (s32[]{:T(128)}, f32[2,4,128]{2,1,0:T(4,128)S(1)}, f32[2,4,128]{2,1,0:T(4,128)S(1)}, f32[2,4,128,128]{3,2,1,0:T(8,128)S(1)}, s32[]{:T(128)}, /*inde...) while((s32[]{:T(128)}, f32[2,4,128]{2,1,0:T(4,128)S(1)}, ...), condition=%wide.region_14.14_spmd, body=%wide.region_9.13_spmd.sunk | while | flops 68569240 | bytes 3148358 | solution.py:142
  1582.3 1.6 conditional.4
  1590.8 1.6 conditional.4
  1598.6 39.9 %while.107 = (s32[]{:T(128)}, f32[2,4,128]{2,1,0:T(4,128)S(1)}, f32[2,4,128]{2,1,0:T(4,128)S(1)}, f32[2,4,128,128]{3,2,1,0:T(8,128)S(1)}, s32[]{:T(128)}, /*inde...) while((s32[]{:T(128)}, f32[2,4,128]{2,1,0:T(4,128)S(1)}, ...), condition=%wide.region_14.14_spmd, body=%wide.region_9.13_spmd.sunk | while | flops 68569240 | bytes 3148358 | solution.py:142
  1628.4 1.6 conditional.4
  1636.9 1.6 conditional.4
  1639.4 4.6 copy.27
  1644.0 11.6 pad_maximum_fusion
  1655.6 272.3 %reduce-scatter.2.cloned.1.call-done = f32[2,2,4,128,129]{4,3,2,1,0:T(8,128)} async-done(((f32[16,2,4,128,129]{4,3,2,1,0:T(8,128)}), f32[2,2,4,128,129]{4,3,2,1,0:T(8,128)}) %reduce-scatter.2.cloned.1.call-update) | async-done | bytes 1056784 | tf_op jit(solution)/shard_map/reduce_scatter | solution.py:33
  1927.9 1.6 slice_reduce_fusion
  1929.5 1.6 fusion.26
  (2845 shorter events, 862.8 us)
Async XLA Ops:
  6.5 120.4 %copy-start = (s32[128]{0:T(128)S(1)}, s32[128]{0:T(128)}, u32[]{:S(2)}) copy-start(s32[128]{0:T(128)} %param.19) | copy-start | bytes 1540
  6.5 60.5 %all-gather.5.cloned.1.call-start = ((), (), s32[]{:S(2)}) async-start(), calls=%async_computation.3 | async-start | bytes 2359296 | tf_op jit(solution)/shard_map/all_gather | solution.py:15
  9.2 113.1 %all-gather.3.cloned.1.call-start = ((), (), s32[]{:S(2)}) async-start(), calls=%async_computation.2 | async-start | bytes 4718592 | tf_op jit(solution)/shard_map/all_gather | solution.py:82
  826.3 48.9 %all-to-all-start = ((f32[8,16,2,4,128]{4,1,3,2,0:T(8,128)}), f32[8,16,2,4,128]{4,1,3,2,0:T(8,128)S(1)}, u32[]{:S(2)}, u32[]{:S(2)}) async-start(f32[8,16,2,4,128]{4,1,3,2,0:T(8,128)} %broadcast_in_dim.92), calls=%async_computation | async-start | bytes 1048576 | tf_op jit(solution)/shard_map/all_to_all | solution.py:20
  862.2 1065.7 %reduce-scatter.2.cloned.1.call-start = ((), (), s32[]{:S(2)}) async-start(), calls=%async_computation.4 | async-start | bytes 18874368 | tf_op jit(solution)/shard_map/reduce_scatter | solution.py:33
Sparse Core Ops, SparseCore 0:
  9.3 57.7 all-gather.4
  68.9 53.2 all-gather.2
  1655.7 272.1 reduce-scatter.1
where the time goes:
time: 1980 us; the launch traced here: 1940 us
  loops' own time  911 us (46%)
  local copies, waits for them, and re-layouts  404 us (20%)
  waiting for transfers between devices  395 us (20%)
  matrix products  125 us (6%)
  other arithmetic  55.1 us (3%)
  starting transfers between devices  36 us (2%)
    another operation x16, loops' own time, local_peak(): return lax.fori_loop(0, key_blocks, local_visit_key, start_peak)  328 us
    another operation x16, loops' own time, one_query(): final = lax.fori_loop(0, key_blocks, one_visit_key, begin)  313 us
    dynamic_slice x512, local copies, waits for them, and re-layouts, key_anchor_of(): span_order[(outer_here * inner_count + block_k // 2) * 2 + block_k % 2]  301 us
    reduce_scatter x1, waiting for transfers between devices, sent_together(): whole = lax.psum_scatter(both, axis, scatter_dimension=dim, tiled=True)  272 us
    another operation x256, loops' own time, local_visit_key(): lax.cond(key_anchor <= query_anchor, lambda held: block_peak(held, query_...  86.3 us
    another operation x256, loops' own time, one_visit_key(): lax.cond(key_anchor <= query_anchor, lambda carried: attend_block(carried...  82 us
    dot_general x129, matrix products, attend_block(): jnp.einsum('ghqk,kga->ghqa', weights.astype(jnp.bfloat16), value_tile, pr...  59.1 us
    all_gather x1, waiting for transfers between devices, in_one_piece(): lax.all_gather(both, axis, axis=dim, tiled=True)  55.9 us
  transfers between devices with their start and end apart: 4, of which 4 were waited for; matrix products, arithmetic and copies ran while one was open for 0% of the time, Pallas kernels for 0%

commit v1 on v0

v1 whole, which is shorter than its diff:
```python
import math

import jax
import jax.numpy as jnp
from jax import lax
from jax.experimental import pallas as pl
from jax.experimental.pallas import tpu as pltpu
from jax.sharding import PartitionSpec as P

CHUNK = 512
ROW = 4
RING = 8
MESH = pl.DeviceIdType.MESH


def place():
    outer, inner = lax.axis_index("outer"), lax.axis_index("inner")
    return inner // 2, outer // 2 * 2 + inner % 2, outer % 2, lax.axis_index("head")


def device(x, z, c, y):
    return (z // 2 * 2 + c, x * 2 + z % 2, y)


def greet(peers):
    barrier = pltpu.get_barrier_semaphore()
    for peer in peers:
        pl.semaphore_signal(barrier, inc=1, device_id=peer, device_id_type=MESH)
    pl.semaphore_wait(barrier, len(peers))


def row_mates(x, z, c, y):
    steps = [(dx, dc) for dx in range(ROW) for dc in range(2) if (dx, dc) != (0, 0)]
    return steps, [device((x + dx) % ROW, z, (c + dc) % 2, y) for dx, dc in steps]


def gather_kernel(q_ref, kv_ref, q_all, kv_all, q_send, q_recv, x_send, x_recv, up_send, up_recv,
                  down_send, down_recv, core_send, core_recv, own_sem):
    x, z, c, y = place()
    steps, mates = row_mates(x, z, c, y)
    above, below = device(x, (z + 1) % RING, c, y), device(x, (z + RING - 1) % RING, c, y)
    partner = device(x, z, 1 - c, y)
    greet([*mates, above, below])

    def remote(src, dst, send, recv, to):
        return pltpu.make_async_remote_copy(
            src_ref=src, dst_ref=dst, send_sem=send, recv_sem=recv, device_id=to, device_id_type=MESH)

    started = []
    role = x % 2 * 2 + x // 2
    mine = kv_ref.at[role]
    keep_kv = pltpu.make_async_copy(mine, kv_all.at[c, z, x], own_sem.at[0])
    keep_q = pltpu.make_async_copy(q_ref.at[x % 2, c], q_all.at[x, c], own_sem.at[1])

    def pass_up(t, j, src):
        slot = kv_all.at[c, (z - t + RING) % RING, (x + j) % ROW]
        copy = remote(src, slot, up_send.at[t, j], up_recv.at[t, j], above)
        copy.start()
        started.append(copy)

    def pass_down(t, j, src):
        slot = kv_all.at[c, (z + t) % RING, (x + j) % ROW]
        copy = remote(src, slot, down_send.at[t, j], down_recv.at[t, j], below)
        copy.start()
        started.append(copy)

    def to_partner(r, j, src):
        slot = kv_all.at[c, (z + r) % RING, (x + j) % ROW]
        copy = remote(src, slot, core_send.at[r, j], core_recv.at[r, j], partner)
        copy.start()
        started.append(copy)

    pass_up(0, 0, mine)
    pass_down(0, 0, mine)
    for d in (1, 3, 2):
        to = (x + d) % ROW
        copy = remote(kv_ref.at[to % 2 * 2 + to // 2], kv_all.at[c, z, x], x_send.at[d], x_recv.at[d],
                      device(to, z, c, y))
        copy.start()
        started.append(copy)
    to_partner(0, 0, mine)
    keep_kv.start()
    keep_q.start()
    for n, (dx, dc) in enumerate(steps):
        to = (x + dx) % ROW
        copy = remote(q_ref.at[to % 2, (c + dc) % 2], q_all.at[x, c], q_send.at[n], q_recv.at[n], mates[n])
        copy.start()
        started.append(copy)

    def arrived(dst, recv):
        remote(dst, dst, x_send.at[0], recv, partner).wait_recv()

    for j in (1, 3, 2):
        slot = kv_all.at[c, z, (x + j) % ROW]
        arrived(slot, x_recv.at[ROW - j])
        pass_up(0, j, slot)
        pass_down(0, j, slot)
        to_partner(0, j, slot)
    for t in range(1, RING // 2 + 1):
        last = t == RING // 2
        for j in (0, 1, 3, 2):
            if not last or j in (0, 1):
                slot = kv_all.at[c, (z - t + RING) % RING, (x + j) % ROW]
                arrived(slot, up_recv.at[t - 1, j])
                if t < RING // 2 - 1 or (t == RING // 2 - 1 and j in (0, 1)):
                    pass_up(t, j, slot)
                to_partner((RING - t) % RING, j, slot)
            if not last or j in (2, 3):
                slot = kv_all.at[c, (z + t) % RING, (x + j) % ROW]
                arrived(slot, down_recv.at[t - 1, j])
                if t < RING // 2 - 1 or (t == RING // 2 - 1 and j in (2, 3)):
                    pass_down(t, j, slot)
                to_partner(t, j, slot)
    for n, (dx, dc) in enumerate(steps):
        arrived(q_all.at[(x + ROW - dx) % ROW, (c + dc) % 2], q_recv.at[n])
    for r in range(RING):
        for j in range(ROW):
            arrived(kv_all.at[1 - c, (z + r) % RING, (x + j) % ROW], core_recv.at[r, j])
    keep_kv.wait()
    keep_q.wait()
    for copy in started:
        copy.wait_send()


def gather(q, kv):
    sem = pltpu.SemaphoreType.DMA
    half_ring = RING // 2
    vmem = pl.BlockSpec(memory_space=pltpu.VMEM)
    return pl.pallas_call(
        gather_kernel,
        out_shape=(jax.ShapeDtypeStruct((ROW, 2, *q.shape[2:]), q.dtype),
                   jax.ShapeDtypeStruct((2, RING, ROW, *kv.shape[1:]), kv.dtype)),
        in_specs=[vmem, vmem],
        out_specs=(vmem, vmem),
        scratch_shapes=[
            sem((2 * ROW - 1,)), sem((2 * ROW - 1,)), sem((ROW,)), sem((ROW,)),
            sem((half_ring, ROW)), sem((half_ring, ROW)), sem((half_ring, ROW)), sem((half_ring, ROW)),
            sem((RING, ROW)), sem((RING, ROW)), sem((2,)),
        ],
        compiler_params=pltpu.CompilerParams(
            collective_id=0, has_side_effects=True, vmem_limit_bytes=32 * 1024 * 1024),
        cost_estimate=pl.CostEstimate(flops=0, bytes_accessed=20_000_000, transcendentals=0),
    )(q, kv)


def attend_kernel(half_ref, q_pos, k_pos, q_ref, kv_ref, o_ref, lse_ref,
                  k_sorted, v_sorted, v_turned, s_even, s_odd, acc, top, total):
    groups, _, each, piece, width = kv_ref.shape
    tiles, lanes, _ = q_ref.shape
    block = 2 * piece
    per_chunk = CHUNK // piece
    rate = math.log2(math.e) / math.sqrt(width)
    half = half_ref[0]

    def put(g, c):
        for b in range(each):
            at = pl.multiple_of(k_pos[g * each + b] * piece, piece)
            k_sorted[pl.ds(at, piece), :] = kv_ref[g, 0, b]
            v_sorted[pl.ds(at, piece), :] = kv_ref[g, 1, b]
        return c

    lax.fori_loop(0, groups, put, 0, unroll=2)

    def turn(g, c):
        at = pl.multiple_of(g * CHUNK, CHUNK)
        v_turned[:, pl.ds(at, CHUNK)] = v_sorted[pl.ds(at, CHUNK), :].T
        return c

    lax.fori_loop(0, groups * each * piece // CHUNK, turn, 0)

    def scores(j, t, out):
        at = pl.multiple_of(j * CHUNK, CHUNK)
        out[...] = lax.dot_general(
            k_sorted[pl.ds(at, CHUNK), :], q_ref[t], (((1,), (1,)), ((), ())),
            preferred_element_type=jnp.float32)

    def absorb(j, s):
        at = pl.multiple_of(j * CHUNK, CHUNK)
        old = top[...]
        new = jnp.maximum(old, jnp.max(s, axis=0, keepdims=True))
        p = jnp.exp2((s - new) * rate)
        fade = jnp.exp2((old - new) * rate)
        top[...] = new
        total[...] = total[...] * fade + jnp.sum(p, axis=0, keepdims=True)
        acc[...] = acc[...] * fade + jnp.dot(
            v_turned[:, pl.ds(at, CHUNK)], p.astype(jnp.bfloat16),
            preferred_element_type=jnp.float32)

    def tile(t, c):
        pos = q_pos[t]
        full = pos // per_chunk
        top[...] = jnp.full_like(top, -1e30)
        total[...] = jnp.zeros_like(total)
        acc[...] = jnp.zeros_like(acc)
        scores(0, t, s_even)

        def pair(h, c):
            scores(2 * h + 1, t, s_odd)
            absorb(2 * h, s_even[...])
            scores(2 * h + 2, t, s_even)
            absorb(2 * h + 1, s_odd[...])
            return c

        lax.fori_loop(0, full // 2, pair, 0)

        def last(s_buf):
            k_row = lax.broadcasted_iota(jnp.int32, (CHUNK, lanes), 0)
            k_at = (full * per_chunk + k_row // piece) * block + k_row % piece + half * piece
            q_row = lax.broadcasted_iota(jnp.int32, (CHUNK, lanes), 1)
            q_at = pos * block + q_row % block
            absorb(full, jnp.where(k_at <= q_at, s_buf[...], -2e30))

        @pl.when(full % 2 == 1)
        def _():
            scores(full, t, s_odd)
            absorb(full - 1, s_even[...])
            last(s_odd)

        @pl.when(full % 2 == 0)
        def _():
            last(s_even)

        weight = total[...]
        some = weight > 0
        weight = jnp.where(some, weight, 1.0)
        o_ref[t] = (acc[...] * (1.0 / weight)).T.astype(jnp.bfloat16)
        lse_ref[t] = jnp.where(some, top[...] * rate + jnp.log2(weight), -1e30)
        return c

    lax.fori_loop(0, tiles, tile, 0)


def attend(half, q_pos, k_pos, q, kv):
    tiles, lanes, width = q.shape
    groups, _, each, piece, _ = kv.shape
    keys = groups * each * piece
    smem = pl.BlockSpec(memory_space=pltpu.SMEM)
    vmem = pl.BlockSpec(memory_space=pltpu.VMEM)
    return pl.pallas_call(
        attend_kernel,
        out_shape=(jax.ShapeDtypeStruct(q.shape, jnp.bfloat16),
                   jax.ShapeDtypeStruct((tiles, 1, lanes), jnp.float32)),
        in_specs=[smem, smem, smem, vmem, vmem],
        out_specs=(vmem, vmem),
        scratch_shapes=[
            pltpu.VMEM((keys, width), jnp.bfloat16),
            pltpu.VMEM((keys, width), jnp.bfloat16),
            pltpu.VMEM((width, keys), jnp.bfloat16),
            pltpu.VMEM((CHUNK, lanes), jnp.float32),
            pltpu.VMEM((CHUNK, lanes), jnp.float32),
            pltpu.VMEM((width, lanes), jnp.float32),
            pltpu.VMEM((1, lanes), jnp.float32),
            pltpu.VMEM((1, lanes), jnp.float32),
        ],
        compiler_params=pltpu.CompilerParams(vmem_limit_bytes=48 * 1024 * 1024),
    )(half, q_pos, k_pos, q, kv)


def return_kernel(o_ref, lse_ref, o_all, lse_all, o_send, o_recv, l_send, l_recv, own_sem):
    x, z, c, y = place()
    steps, mates = row_mates(x, z, c, y)
    greet(mates)
    keep = [pltpu.make_async_copy(o_ref.at[x, c], o_all.at[x, c], own_sem.at[0]),
            pltpu.make_async_copy(lse_ref.at[x, c], lse_all.at[x, c], own_sem.at[1])]
    copies = []
    for n, (dx, dc) in enumerate(steps):
        to_x, to_c = (x + dx) % ROW, (c + dc) % 2
        for src, dst, send, recv in ((lse_ref, lse_all, l_send, l_recv), (o_ref, o_all, o_send, o_recv)):
            copy = pltpu.make_async_remote_copy(
                src_ref=src.at[to_x, to_c], dst_ref=dst.at[x, c], send_sem=send.at[n], recv_sem=recv.at[n],
                device_id=mates[n], device_id_type=MESH)
            copy.start()
            copies.append(copy)
    for copy in keep:
        copy.start()
    for copy in keep:
        copy.wait()
    for copy in copies:
        copy.wait()


def send_back(o, lse):
    sem = pltpu.SemaphoreType.DMA
    vmem = pl.BlockSpec(memory_space=pltpu.VMEM)
    n = 2 * ROW - 1
    return pl.pallas_call(
        return_kernel,
        out_shape=(jax.ShapeDtypeStruct(o.shape, o.dtype), jax.ShapeDtypeStruct(lse.shape, lse.dtype)),
        in_specs=[vmem, vmem],
        out_specs=(vmem, vmem),
        scratch_shapes=[sem((n,)), sem((n,)), sem((n,)), sem((n,)), sem((2,))],
        compiler_params=pltpu.CompilerParams(
            collective_id=1, has_side_effects=True, vmem_limit_bytes=32 * 1024 * 1024),
        cost_estimate=pl.CostEstimate(flops=0, bytes_accessed=20_000_000, transcendentals=0),
    )(o, lse)


def body(stored_query_rows, stored_key_rows, stored_value_rows, span_order):
    rows, heads, width = stored_query_rows.shape
    each = 2
    span = rows // each
    x, z, c, _ = place()
    q = stored_query_rows.reshape(each, span, 2, 2, 2, width).transpose(2, 3, 0, 4, 1, 5)
    q = q.reshape(2, 2, each, 2 * span, width)
    kv = jnp.stack([stored_key_rows, stored_value_rows])
    kv = kv.reshape(2, each, 2, span // 2, 2, width).transpose(4, 2, 0, 1, 3, 5)
    kv = kv.reshape(4, 2, each, span // 2, width)
    q_all, kv_all = gather(q, kv)

    order = span_order.reshape(RING // 2, 2, ROW, 2, each)
    k_pos = order.transpose(1, 0, 3, 2, 4).reshape(-1)
    in_row = lax.dynamic_index_in_dim(lax.dynamic_index_in_dim(order, z // 2, 0, False), z % 2, 2, False)
    q_pos = in_row.transpose(1, 0, 2).reshape(-1)
    half = jnp.reshape(x // 2, (1,)).astype(jnp.int32)
    o, lse = attend(half, q_pos, k_pos, q_all.reshape(2 * ROW * each, 2 * span, width),
                    kv_all.reshape(2 * RING * ROW, 2, each, span // 2, width))

    o, lse = send_back(o.reshape(ROW, 2, each, 2 * span, width), lse.reshape(ROW, 2, each, 1, 2 * span))
    o = o.reshape(2, 2, 2, each, 2, span, width)
    lse = lse.reshape(2, 2, 2, each, 2, span)
    top = jnp.max(lse, axis=0)
    weights = jnp.exp2(lse - top)
    share = weights / jnp.sum(weights, axis=0)
    result = jnp.sum(o.astype(jnp.float32) * share[..., None], axis=0).astype(jnp.bfloat16)
    return result.transpose(2, 4, 0, 1, 3, 5).reshape(rows, heads, width)


def solution(mesh):
    placed = (
        P(("outer", "inner"), "head", None),
        P(("outer", "inner"), "head", None),
        P(("outer", "inner"), "head", None),
        P(),
    )
    return jax.shard_map(
        body,
        mesh=mesh,
        in_specs=placed,
        out_specs=P(("outer", "inner"), "head", None),
        check_vma=False,
    )
```

time: 1980 us -> 115 us (0.06)
  the two profiles are of different devices: /device:TPU:1 before, /device:TPU:97 now
where the time goes in v1:
time: 115 us; the launch traced here: 116 us
  Pallas kernels  108 us (94%)
  local copies, waits for them, and re-layouts  7.16 us (6%)
    pallas_call x1, Pallas kernels, attend(): pl.pallas_call(attend_kernel, out_shape=(jax.ShapeDtypeStruct(q.shape, jn...  56.9 us
    pallas_call x1, Pallas kernels, gather(): pl.pallas_call(gather_kernel, out_shape=(jax.ShapeDtypeStruct((ROW, 2, *q...  33 us
    pallas_call x1, Pallas kernels, send_back(): pl.pallas_call(return_kernel, out_shape=(jax.ShapeDtypeStruct(o.shape, o....  18.1 us

profile of v1, /device:TPU:97, one launch (start us, length us, event | category | flops | bytes accessed | tf_op | source)
XLA Modules:
  0.0 116.2 jit_solution(11776169223837568194)
XLA Ops:
  0.0 0.8 reshape.64
  0.9 0.1 reshape.65.q_pos
  1.0 0.1 reshape.66.k_pos
  1.1 0.9 copy.27
  2.0 0.9 copy.28
  3.0 1.1 copy.26
  4.1 33.0 %shard_map.46 = (bf16[4,2,2,256,128]{4,3,2,1,0:T(8,128)(2,1)S(1)}, bf16[2,8,4,2,2,64,128]{6,5,4,3,2,1,0:T(8,128)(2,1)S(1)}) custom-call(bf16[2,2,2,256,128]{4,3,2,1,0:T(8,128)(2,1)S(1)} %bitcast.28, bf16[4,2,2,64,128]{4,3,2,1,0:T(8,128)(2,1)S(1)} %bitcast.29), custom_call_target="tpu_custom_call" | custom-call | bytes 20000000 | tf_op jit(solution)/shard_map/pallas_call | solution.py:129
  37.2 0.0 copy-start
  37.2 1.9 %copy-done = bf16[2,8,4,2,2,64,128]{6,5,4,3,2,1,0:T(8,128)(2,1)} copy-done((bf16[2,8,4,2,2,64,128]{6,5,4,3,2,1,0:T(8,128)(2,1)}, bf16[2,8,4,2,2,64,128]{6,5,4,3,2,1,0:T(8,128)(2,1)S(1)}, u32[]{:S(2)}) %copy-start) | copy-done | bytes 4194328
  39.1 56.9 %shard_map.47 = (bf16[16,256,128]{2,1,0:T(8,128)(2,1)S(1)}, f32[16,1,256]{2,1,0:T(1,128)S(1)}) custom-call(s32[1]{0:T(128)} %bitcast.half_ref, s32[16]{0:T(128)S(1)} %reshape.65.q_pos, s32[128]{0:T(128)S(1)} %reshape.66.k_pos, bf16[16,256,128]{2,1,0:T(8,128)(2,1)S(1)} %bitcast.32, bf16[64,2,2,64,128]{4,3,2,1,0:T(8,128)(2,1)} %bitcast.27), custom_call_target="tpu_custom_call" | custom-call | tf_op jit(solution)/shard_map/pallas_call | solution.py:239
  96.0 18.1 %shard_map.48 = (bf16[4,2,2,256,128]{4,3,2,1,0:T(8,128)(2,1)S(1)}, f32[4,2,2,1,256]{4,3,2,1,0:T(1,128)S(1)}) custom-call(bf16[4,2,2,256,128]{4,3,2,1,0:T(8,128)(2,1)S(1)} %bitcast.31, f32[4,2,2,1,256]{4,3,2,1,0:T(1,128)S(1)} %bitcast.36), custom_call_target="tpu_custom_call" | custom-call | bytes 20000000 | tf_op jit(solution)/shard_map/pallas_call | solution.py:286
  114.2 0.8 fusion
  115.1 1.1 copy.30
  (8 shorter events, 0.2 us)
Async XLA Ops:
  37.2 1.9 %copy-start = (bf16[2,8,4,2,2,64,128]{6,5,4,3,2,1,0:T(8,128)(2,1)}, bf16[2,8,4,2,2,64,128]{6,5,4,3,2,1,0:T(8,128)(2,1)S(1)}, u32[]{:S(2)}) copy-start(bf16[2,8,4,2,2,64,128]{6,5,4,3,2,1,0:T(8,128)(2,1)S(1)} %get-tuple-element.12) | copy-start | bytes 12582916

commit v2 on v1

--- a/solution.py
+++ b/solution.py
@@ -7,7 +7,8 @@
 from jax.experimental.pallas import tpu as pltpu
 from jax.sharding import PartitionSpec as P
 
-CHUNK = 512
+CHUNK = 1024
+UNROLL = 4
 ROW = 4
 RING = 8
 MESH = pl.DeviceIdType.MESH
@@ -144,90 +145,130 @@
 
 
 def attend_kernel(half_ref, q_pos, k_pos, q_ref, kv_ref, o_ref, lse_ref,
-                  k_sorted, v_sorted, v_turned, s_even, s_odd, acc, top, total):
+                  k_sorted, v_sorted, v_turned, q_turned, p_bufs, acc, top):
     groups, _, each, piece, width = kv_ref.shape
     tiles, lanes, _ = q_ref.shape
     block = 2 * piece
-    per_chunk = CHUNK // piece
     rate = math.log2(math.e) / math.sqrt(width)
     half = half_ref[0]
 
     def put(g, c):
         for b in range(each):
-            at = pl.multiple_of(k_pos[g * each + b] * piece, piece)
+            at = pl.multiple_of(CHUNK + k_pos[g * each + b] * piece, piece)
             k_sorted[pl.ds(at, piece), :] = kv_ref[g, 0, b]
-            v_sorted[pl.ds(at, piece), :] = kv_ref[g, 1, b]
+            v_sorted[pl.ds(at - CHUNK, piece), :] = kv_ref[g, 1, b]
         return c
 
-    lax.fori_loop(0, groups, put, 0, unroll=2)
+    lax.fori_loop(0, groups, put, 0, unroll=4)
+    first = k_sorted[CHUNK:CHUNK + piece, :]
+    for u in range(0, CHUNK, piece):
+        k_sorted[u:u + piece, :] = first
+    pads = CHUNK // width
+    extra = v_turned.shape[1] - width
+    v_turned[:pads] = jnp.zeros((pads, *v_turned.shape[1:]), v_turned.dtype)
+    v_turned[pads:, width:, :] = jnp.ones((v_turned.shape[0] - pads, extra, width), v_turned.dtype)
 
     def turn(g, c):
-        at = pl.multiple_of(g * CHUNK, CHUNK)
-        v_turned[:, pl.ds(at, CHUNK)] = v_sorted[pl.ds(at, CHUNK), :].T
+        at = pl.multiple_of(g * width, width)
+        v_turned[pads + g, :width, :] = v_sorted[pl.ds(at, width), :].T
         return c
 
-    lax.fori_loop(0, groups * each * piece // CHUNK, turn, 0)
-
-    def scores(j, t, out):
-        at = pl.multiple_of(j * CHUNK, CHUNK)
-        out[...] = lax.dot_general(
-            k_sorted[pl.ds(at, CHUNK), :], q_ref[t], (((1,), (1,)), ((), ())),
-            preferred_element_type=jnp.float32)
-
-    def absorb(j, s):
-        at = pl.multiple_of(j * CHUNK, CHUNK)
-        old = top[...]
-        new = jnp.maximum(old, jnp.max(s, axis=0, keepdims=True))
-        p = jnp.exp2((s - new) * rate)
-        fade = jnp.exp2((old - new) * rate)
-        top[...] = new
-        total[...] = total[...] * fade + jnp.sum(p, axis=0, keepdims=True)
-        acc[...] = acc[...] * fade + jnp.dot(
-            v_turned[:, pl.ds(at, CHUNK)], p.astype(jnp.bfloat16),
-            preferred_element_type=jnp.float32)
-
-    def tile(t, c):
-        pos = q_pos[t]
-        full = pos // per_chunk
-        top[...] = jnp.full_like(top, -1e30)
-        total[...] = jnp.zeros_like(total)
-        acc[...] = jnp.zeros_like(acc)
-        scores(0, t, s_even)
-
-        def pair(h, c):
-            scores(2 * h + 1, t, s_odd)
-            absorb(2 * h, s_even[...])
-            scores(2 * h + 2, t, s_even)
-            absorb(2 * h + 1, s_odd[...])
+    lax.fori_loop(0, groups * each * piece // width, turn, 0, unroll=8)
+
+    def twice(k):
+        return jnp.concatenate([k, k], axis=1)
+
+    k_row = lax.broadcasted_iota(jnp.int32, (block, lanes), 0)
+    q_row = lax.broadcasted_iota(jnp.int32, (block, lanes), 1)
+    lag = k_row // piece * block + k_row % piece - q_row % block
+
+    def score(into, group, keys):
+        at = pl.multiple_of(group * width, width)
+        return jnp.dot(twice(k_sorted[pl.ds(at, keys), :]), q_turned[into], preferred_element_type=jnp.float32)
+
+    def start(t, items):
+        q = (q_ref[t].astype(jnp.float32) * rate).T
+        high = q.astype(jnp.bfloat16)
+        q_turned[t, :width, :] = high
+        q_turned[t, width:, :] = (q - high.astype(jnp.float32)).astype(jnp.bfloat16)
+        own = q_pos[t] // 2
+        s = score(t, pads + own, block)
+        s = jnp.where(lag <= q_pos[t] % 2 * block - half * piece, s, -2e30)
+        peak = jnp.maximum(jnp.max(s, axis=0, keepdims=True), -1e30)
+        early = jnp.max(score(t, 0, piece), axis=0, keepdims=True)
+        peak = jnp.where(own > 0, jnp.maximum(peak, early), peak)
+        top[t] = peak
+        acc[t] = jnp.dot(v_turned[pads + own], jnp.exp2(s - peak).astype(jnp.bfloat16),
+                         preferred_element_type=jnp.float32)
+        return items + jnp.maximum((own + pads - 1) // pads, 1)
+
+    items = lax.fori_loop(0, tiles, start, 0, unroll=4)
+    q_turned[tiles] = jnp.zeros(q_turned.shape[1:], q_turned.dtype)
+    top[tiles] = jnp.zeros(top.shape[1:], jnp.float32)
+    acc[tiles] = jnp.zeros(acc.shape[1:], jnp.float32)
+
+    def where_is(t, w):
+        own = jnp.where(t < tiles, q_pos[jnp.minimum(t, tiles - 1)] // 2, 0)
+        into = jnp.where(own > 0, t, tiles)
+        group = jnp.maximum(own - w * pads, 0)
+        return into, group, own <= (w + 1) * pads
+
+    def values(group):
+        return jnp.concatenate([v_turned[group + i] for i in range(pads)], axis=1)
+
+    def weigh(into, group, slot):
+        p_bufs[slot][...] = jnp.exp2(score(into, group, CHUNK) - top[into]).astype(jnp.bfloat16)
+
+    def absorb(into, group, slot):
+        acc[into] += jnp.dot(values(group), p_bufs[slot][...], preferred_element_type=jnp.float32)
+
+    def steps(n, at):
+        t, w = at
+        for u in range(UNROLL):
+            into, group, last = where_is(t, w)
+            t, w = jnp.where(last, t + 1, t), jnp.where(last, 0, w + 1)
+            ahead, ahead_group, _ = where_is(t, w)
+            weigh(ahead, ahead_group, 1 - u % 2)
+            absorb(into, group, u % 2)
+        return t, w
+
+    begin, begin_group, _ = where_is(jnp.int32(0), jnp.int32(0))
+    weigh(begin, begin_group, 0)
+    lax.fori_loop(0, (items + UNROLL - 1) // UNROLL, steps, (jnp.int32(0), jnp.int32(0)))
+
+    def again(t, c):
+        start(t, 0)
+        own = q_pos[t] // 2
+
+        def window(w, c):
+            group = own - w * pads
+            s = score(t, group, CHUNK)
+            old = top[t]
+            new = jnp.maximum(old, jnp.max(s, axis=0, keepdims=True))
+            top[t] = new
+            acc[t] = acc[t] * jnp.exp2(old - new) + jnp.dot(
+                values(group), jnp.exp2(s - new).astype(jnp.bfloat16), preferred_element_type=jnp.float32)
             return c
 
-        lax.fori_loop(0, full // 2, pair, 0)
-
-        def last(s_buf):
-            k_row = lax.broadcasted_iota(jnp.int32, (CHUNK, lanes), 0)
-            k_at = (full * per_chunk + k_row // piece) * block + k_row % piece + half * piece
-            q_row = lax.broadcasted_iota(jnp.int32, (CHUNK, lanes), 1)
-            q_at = pos * block + q_row % block
-            absorb(full, jnp.where(k_at <= q_at, s_buf[...], -2e30))
-
-        @pl.when(full % 2 == 1)
-        def _():
-            scores(full, t, s_odd)
-            absorb(full - 1, s_even[...])
-            last(s_odd)
-
-        @pl.when(full % 2 == 0)
-        def _():
-            last(s_even)
-
-        weight = total[...]
+        return lax.fori_loop(0, (own + pads - 1) // pads, window, c)
+
+    most = acc[0, width:width + 8, :]
+    for t in range(1, tiles):
+        most = jnp.maximum(most, acc[t, width:width + 8, :])
+
+    @pl.when(jnp.logical_not(jnp.max(most) < 2.0 ** 80))
+    def _():
+        lax.fori_loop(0, tiles, again, 0)
+
+    def finish(t, c):
+        weight = acc[t, pl.ds(width, 1), :]
         some = weight > 0
         weight = jnp.where(some, weight, 1.0)
-        o_ref[t] = (acc[...] * (1.0 / weight)).T.astype(jnp.bfloat16)
-        lse_ref[t] = jnp.where(some, top[...] * rate + jnp.log2(weight), -1e30)
+        o_ref[t] = (acc[t, :width, :] * (1.0 / weight)).T.astype(jnp.bfloat16)
+        lse_ref[t] = jnp.where(some, top[t] + jnp.log2(weight), -1e30)
         return c
 
-    lax.fori_loop(0, tiles, tile, 0)
+    lax.fori_loop(0, tiles, finish, 0, unroll=4)
 
 
 def attend(half, q_pos, k_pos, q, kv):
@@ -243,16 +284,15 @@
         in_specs=[smem, smem, smem, vmem, vmem],
         out_specs=(vmem, vmem),
         scratch_shapes=[
+            pltpu.VMEM((CHUNK + keys, width), jnp.bfloat16),
             pltpu.VMEM((keys, width), jnp.bfloat16),
-            pltpu.VMEM((keys, width), jnp.bfloat16),
-            pltpu.VMEM((width, keys), jnp.bfloat16),
-            pltpu.VMEM((CHUNK, lanes), jnp.float32),
-            pltpu.VMEM((CHUNK, lanes), jnp.float32),
-            pltpu.VMEM((width, lanes), jnp.float32),
-            pltpu.VMEM((1, lanes), jnp.float32),
-            pltpu.VMEM((1, lanes), jnp.float32),
+            pltpu.VMEM(((CHUNK + keys) // width, width + 16, width), jnp.bfloat16),
+            pltpu.VMEM((tiles + 1, 2 * width, lanes), jnp.bfloat16),
+            [pltpu.VMEM((CHUNK, lanes), jnp.bfloat16)] * 2,
+            pltpu.VMEM((tiles + 1, width + 16, lanes), jnp.float32),
+            pltpu.VMEM((tiles + 1, 1, lanes), jnp.float32),
         ],
-        compiler_params=pltpu.CompilerParams(vmem_limit_bytes=48 * 1024 * 1024),
+        compiler_params=pltpu.CompilerParams(vmem_limit_bytes=26 * 1024 * 1024),
     )(half, q_pos, k_pos, q, kv)
 
 

time: 115 us -> 88.1 us (0.77)
  the two profiles are of different devices: /device:TPU:97 before, /device:TPU:33 now
where the time goes in v2:
time: 88.1 us; the launch traced here: 88.8 us
  Pallas kernels  82.5 us (94%)
  local copies, waits for them, and re-layouts  5.24 us (6%)
  other arithmetic  0.91 us (1%)
    pallas_call x1, Pallas kernels, gather(): pl.pallas_call(gather_kernel, out_shape=(jax.ShapeDtypeStruct((ROW, 2, *q...  33.6 us
    pallas_call x1, Pallas kernels, attend(): pl.pallas_call(attend_kernel, out_shape=(jax.ShapeDtypeStruct(q.shape, jn...  29.2 us
    pallas_call x1, Pallas kernels, send_back(): pl.pallas_call(return_kernel, out_shape=(jax.ShapeDtypeStruct(o.shape, o....  19.8 us
    another operation x2, local copies, waits for them, and re-layouts, body(): kv = jnp.stack([stored_key_rows, stored_value_rows])  1.85 us

profile of v2, /device:TPU:33, one launch (start us, length us, event | category | flops | bytes accessed | tf_op | source)
XLA Modules:
  0.0 88.8 jit_solution(1661709750503839180)
XLA Ops:
  0.0 0.8 reshape.64
  0.9 0.1 reshape.65.q_pos
  1.0 0.1 reshape.66.k_pos
  1.1 0.9 %copy.27 = bf16[1,2,2,64,2,128]{5,3,1,0,2,4:T(8,128)(2,1)S(1)} copy(bf16[1,2,2,64,2,128]{5,4,3,2,1,0:T(2,128)(2,1)} %bitcast.41) | data formatting | bytes 262144 | tf_op jit(solution)/shard_map/stack | solution.py:345
  2.0 0.9 %copy.28 = bf16[1,2,2,64,2,128]{5,3,1,0,2,4:T(8,128)(2,1)S(1)} copy(bf16[1,2,2,64,2,128]{5,4,3,2,1,0:T(2,128)(2,1)} %bitcast.42) | data formatting | bytes 262144 | tf_op jit(solution)/shard_map/stack | solution.py:345
  3.0 1.1 %copy.26 = bf16[2,128,2,2,2,128]{5,1,4,0,3,2:T(8,128)(2,1)S(1)} copy(bf16[2,128,2,2,2,128]{5,4,3,2,1,0:T(2,128)(2,1)} %bitcast.39) | data formatting | bytes 1048576 | tf_op jit(solution)/shard_map/reshape | solution.py:343
  4.1 33.6 %shard_map.46 = (bf16[4,2,2,256,128]{4,3,2,1,0:T(8,128)(2,1)S(1)}, bf16[2,8,4,2,2,64,128]{6,5,4,3,2,1,0:T(8,128)(2,1)S(1)}) custom-call(bf16[2,2,2,256,128]{4,3,2,1,0:T(8,128)(2,1)S(1)} %bitcast.28, bf16[4,2,2,64,128]{4,3,2,1,0:T(8,128)(2,1)S(1)} %bitcast.29), custom_call_target="tpu_custom_call" | custom-call | bytes 20000000 | tf_op jit(solution)/shard_map/pallas_call | solution.py:130
  37.7 29.2 %shard_map.47 = (bf16[16,256,128]{2,1,0:T(8,128)(2,1)S(1)}, f32[16,1,256]{2,1,0:T(1,128)S(1)}) custom-call(s32[1]{0:T(128)} %bitcast.half_ref, s32[16]{0:T(128)S(1)} %reshape.65.q_pos, s32[128]{0:T(128)S(1)} %reshape.66.k_pos, bf16[16,256,128]{2,1,0:T(8,128)(2,1)S(1)} %bitcast.32, bf16[64,2,2,64,128]{4,3,2,1,0:T(8,128)(2,1)S(1)} %bitcast.27), custom_call_target="tpu_custom_call" | custom-call | tf_op jit(solution)/shard_map/pallas_call | solution.py:280
  66.9 19.8 %shard_map.48 = (bf16[4,2,2,256,128]{4,3,2,1,0:T(8,128)(2,1)S(1)}, f32[4,2,2,1,256]{4,3,2,1,0:T(1,128)S(1)}) custom-call(bf16[4,2,2,256,128]{4,3,2,1,0:T(8,128)(2,1)S(1)} %bitcast.31, f32[4,2,2,1,256]{4,3,2,1,0:T(1,128)S(1)} %bitcast.36), custom_call_target="tpu_custom_call" | custom-call | bytes 20000000 | tf_op jit(solution)/shard_map/pallas_call | solution.py:326
  86.8 0.8 fusion
  87.6 1.1 %copy.30 = bf16[256,8,128]{2,1,0:T(8,128)(2,1)} copy(bf16[256,8,128]{2,0,1:T(8,128)(2,1)S(1)} %bitcast.38) | data formatting | bytes 1048576 | tf_op jit(solution)/shard_map/reshape | solution.py:365
  (8 shorter events, 0.2 us)

commit v3 on v1

v3 whole, which is shorter than its diff:
```python
import math

import jax
import jax.numpy as jnp
from jax import lax
from jax.experimental import pallas as pl
from jax.experimental.pallas import tpu as pltpu
from jax.sharding import PartitionSpec as P

ROW = 4
RING = 8
EACH = 2
MESH = pl.DeviceIdType.MESH
NEVER = 2.0**20


def place():
    outer, inner = lax.axis_index("outer"), lax.axis_index("inner")
    return inner // 2, outer // 2 * 2 + inner % 2, outer % 2, lax.axis_index("head")


def device(x, z, c, y):
    return (z // 2 * 2 + c, x * 2 + z % 2, y)


def greet(peers):
    barrier = pltpu.get_barrier_semaphore()
    for peer in peers:
        pl.semaphore_signal(barrier, inc=1, device_id=peer, device_id_type=MESH)
    pl.semaphore_wait(barrier, len(peers))


def row_mates(x, z, c, y):
    steps = [(dx, dc) for dx in range(ROW) for dc in range(2) if (dx, dc) != (0, 0)]
    return steps, [device((x + dx) % ROW, z, (c + dc) % 2, y) for dx, dc in steps]


def remote(src, dst, send, recv, to):
    return pltpu.make_async_remote_copy(
        src_ref=src, dst_ref=dst, send_sem=send, recv_sem=recv, device_id=to, device_id_type=MESH)


def attend_kernel(place_ref, q_ref, kv_ref, q_all, kv_all, acc, top,
                  v_turned, q_turned, marks, p_bufs, relay,
                  q_send, q_recv, far_send, far_recv, on_send, on_recv, x_send, x_recv,
                  up_send, up_recv, down_send, down_recv, core_send, core_recv, own_sem):
    x, z, c, y = place()
    steps, mates = row_mates(x, z, c, y)
    mate = dict(zip(steps, mates))
    above, below = device(x, (z + 1) % RING, c, y), device(x, (z + RING - 1) % RING, c, y)
    partner = mate[0, 1]
    greet([*mates, above, below])
    piece, width = kv_ref.shape[-2:]
    block = 2 * piece
    lanes = q_ref.shape[-2]
    tiles = 2 * ROW * EACH
    window = 2 * ROW * EACH * piece
    rate = math.log2(math.e) / math.sqrt(width)
    half = x // 2
    role = x % 2 * 2 + x // 2
    mine = kv_ref.at[role]

    def slot_of(off, j):
        return kv_all.at[c, (z + off + RING) % RING, (x + j) % ROW]

    def pass_up(t, j, src):
        remote(src, slot_of(-t, j), up_send.at[t, j], up_recv.at[t, j], above).start()

    def pass_down(t, j, src):
        remote(src, slot_of(t, j), down_send.at[t, j], down_recv.at[t, j], below).start()

    def to_partner(off, j, src):
        r = (off + RING) % RING
        remote(src, slot_of(off, j), core_send.at[r, j], core_recv.at[r, j], partner).start()

    def arrived(dst, recv):
        remote(dst, dst, x_send.at[1], recv, partner).wait_recv()

    def gone(src, send):
        remote(src, src, send, x_recv.at[1], partner).wait_send()

    pass_up(0, 0, mine)
    pass_down(0, 0, mine)
    for d in (1, 3, 2):
        to = (x + d) % ROW
        remote(kv_ref.at[to % 2 * 2 + to // 2], kv_all.at[c, z, x], x_send.at[d], x_recv.at[d],
               device(to, z, c, y)).start()
    to_partner(0, 0, mine)
    keep_kv = pltpu.make_async_copy(mine, kv_all.at[c, z, x], own_sem.at[0])
    keep_q = pltpu.make_async_copy(q_ref.at[x % 2, c], q_all.at[x, c], own_sem.at[1])
    keep_kv.start()
    keep_q.start()
    for side, dx in ((0, 1), (1, 3)):
        for dc in range(2):
            remote(q_ref.at[x % 2, (c + dc) % 2, side], relay.at[side, dc], far_send.at[side, dc],
                   far_recv.at[side, dc], mate[dx, 0]).start()
    for n, (dx, dc) in enumerate(steps):
        if dx != 2:
            remote(q_ref.at[(x + dx) % 2, (c + dc) % 2], q_all.at[x, c], q_send.at[n], q_recv.at[n],
                   mates[n]).start()

    k_row = lax.broadcasted_iota(jnp.int32, (window, width), 0)
    column = lax.broadcasted_iota(jnp.int32, (window, width), 1)
    marks[...] = jnp.where((column == k_row // piece) | (column == tiles), 1.0, 0.0).astype(marks.dtype)
    q_turned[:, width + tiles:, :] = jnp.zeros((tiles, width - tiles, lanes), q_turned.dtype)
    v_turned[:, width:, :] = jnp.ones((v_turned.shape[0], v_turned.shape[1] - width, width), v_turned.dtype)

    for j in (1, 3, 2):
        slot = slot_of(0, j)
        arrived(slot, x_recv.at[ROW - j])
        pass_up(0, j, slot)
        pass_down(0, j, slot)
        to_partner(0, j, slot)
    for side, dx in ((0, 1), (1, 3)):
        for dc in range(2):
            arrived(relay.at[side, dc], far_recv.at[side, dc])
            remote(relay.at[side, dc], q_all.at[(x + ROW - dx) % ROW, c, side], on_send.at[side, dc],
                   on_recv.at[side, dc], mate[dx, dc]).start()
    keep_kv.wait()
    keep_q.wait()

    def ready(zc):
        r = (zc - z + RING) % RING
        for j in range(ROW):
            arrived(kv_all.at[1 - c, zc, (x + j) % ROW], core_recv.at[r, j])
        for core in range(2):
            for at in range(ROW):
                v = kv_all[core, zc, at, 1].reshape(EACH * piece, width)
                v_turned[(core * RING + zc) * ROW + at, :width, :] = v.T

    ready(z)

    own_k = lax.broadcasted_iota(jnp.int32, (piece, lanes), 0) + half * piece
    own_allowed = own_k <= lax.broadcasted_iota(jnp.int32, (piece, lanes), 1) % block

    def take(at, core):
        for b in range(EACH):
            t = (at * 2 + core) * EACH + b
            q = q_all[at, core, b].T
            q_turned[t, :width, :] = q
            s = jnp.dot(kv_all[core, z, at, 0, b], q, preferred_element_type=jnp.float32)
            ref = jnp.max(s, axis=0, keepdims=True).astype(jnp.bfloat16).astype(jnp.float32)
            top[t] = ref
            first = lax.broadcasted_iota(jnp.int32, (tiles, lanes), 0) == 0
            q_turned[t, width + tiles:width + 2 * tiles, :] = jnp.where(first, -ref, 0.0).astype(q_turned.dtype)
            p = jnp.where(own_allowed, jnp.exp2((s - ref) * rate), 0.0).astype(jnp.bfloat16)
            v = v_turned[(core * RING + z) * ROW + at]
            acc[t] = jnp.dot(v[:, b * piece:(b + 1) * piece], p, preferred_element_type=jnp.float32)

    take(x, c)
    arrived(q_all.at[x, 1 - c], q_recv.at[steps.index((0, 1))])
    take(x, 1 - c)
    for dx in (1, 3):
        for dc in range(2):
            core = (c + dc) % 2
            arrived(q_all.at[(x + ROW - dx) % ROW, core], q_recv.at[steps.index((dx, dc))])
            take((x + ROW - dx) % ROW, core)
    for dc in range(2):
        core = (c + dc) % 2
        for side in range(2):
            arrived(q_all.at[(x + 2) % ROW, core, side], on_recv.at[side, dc])
        take((x + 2) % ROW, core)

    def row_at(n):
        off = jnp.where(n % 2 == 1, -((n + 1) // 2), n // 2)
        return off, (z + off + RING) % RING

    def weigh(t, zc, buf):
        own = (t // EACH % 2 * ROW + t // (2 * EACH)) * EACH + t % EACH
        before = place_ref[zc] < place_ref[z, pl.ds(own, 1), :]
        q_turned[t, width:width + tiles, :] = jnp.where(before, 0.0, -NEVER).astype(q_turned.dtype)
        k = [kv_all[core, zc, at, 0].reshape(EACH * piece, width) for core in range(2) for at in range(ROW)]
        keys = jnp.concatenate([jnp.concatenate(k, axis=0), marks[...]], axis=1)
        s = jnp.dot(keys, q_turned[t], preferred_element_type=jnp.float32)
        p_bufs[buf][...] = jnp.exp2(s * rate).astype(jnp.bfloat16)

    def absorb(t, zc, buf):
        v = [v_turned[(core * RING + zc) * ROW + at] for core in range(2) for at in range(ROW)]
        acc[t] += jnp.dot(jnp.concatenate(v, axis=1), p_bufs[buf][...], preferred_element_type=jnp.float32)

    def relay_on(n, j):
        t = n // 2 + 1
        rising = n % 2 == 0

        @pl.when((n < 6) & rising)
        def _():
            slot = slot_of(-t, j)
            arrived(slot, up_recv.at[t - 1, j])

            @pl.when((t < 3) | (j < 2))
            def _():
                pass_up(t, j, slot)

            to_partner(-t, j, slot)

        @pl.when((n < 6) & jnp.logical_not(rising))
        def _():
            slot = slot_of(t, j)
            arrived(slot, down_recv.at[t - 1, j])

            @pl.when((t < 3) | (j >= 2))
            def _():
                pass_down(t, j, slot)

            to_partner(t, j, slot)

        @pl.when(n == 6)
        def _():
            slot = slot_of(RING // 2, j)
            arrived(slot, up_recv.at[3, j] if j < 2 else down_recv.at[3, j])
            to_partner(RING // 2, j, slot)

    per_turn = 4
    turns = tiles // per_turn

    def turn(m, carry):
        n, i = m // turns, m % turns
        _, zc = row_at(n)
        _, ahead = row_at(jnp.minimum(n + 1, RING - 1))

        @pl.when(i == 0)
        def _():
            relay_on(n, 0)
            relay_on(n, 1)

        @pl.when(i == 1)
        def _():
            relay_on(n, 3)

        @pl.when(i == 2)
        def _():
            relay_on(n, 2)

        @pl.when((i == turns - 1) & (n < RING - 1))
        def _():
            ready(ahead)

        for u in range(per_turn):
            t = i * per_turn + u
            wrap = t == tiles - 1
            weigh(jnp.where(wrap, 0, t + 1), jnp.where(wrap, ahead, zc), 1 - u % 2)
            absorb(t, zc, u % 2)
        return carry

    weigh(0, z, 0)
    lax.fori_loop(0, RING * turns, turn, 0)

    for j in range(ROW):
        for t in range(RING // 2):
            if t < 3 or j < 2:
                gone(slot_of(0, j), up_send.at[t, j])
            if t < 3 or j >= 2:
                gone(slot_of(0, j), down_send.at[t, j])
        for r in range(RING):
            gone(slot_of(0, j), core_send.at[r, j])
        if j:
            gone(slot_of(0, j), x_send.at[j])
    for side in range(2):
        for dc in range(2):
            gone(relay.at[side, dc], far_send.at[side, dc])
            gone(relay.at[side, dc], on_send.at[side, dc])
    for n, (dx, dc) in enumerate(steps):
        if dx != 2:
            gone(q_all.at[x, c], q_send.at[n])


def attend(places, q, kv):
    sem = pltpu.SemaphoreType.DMA
    half_ring = RING // 2
    vmem = pl.BlockSpec(memory_space=pltpu.VMEM)
    lanes, width = q.shape[-2:]
    piece = kv.shape[-2]
    tiles = 2 * ROW * EACH
    window = tiles * piece
    return pl.pallas_call(
        attend_kernel,
        out_shape=(jax.ShapeDtypeStruct((ROW, 2, *q.shape[2:]), q.dtype),
                   jax.ShapeDtypeStruct((2, RING, ROW, *kv.shape[1:]), kv.dtype),
                   jax.ShapeDtypeStruct((tiles, width + 16, lanes), jnp.float32),
                   jax.ShapeDtypeStruct((tiles, 1, lanes), jnp.float32)),
        in_specs=[vmem] * 3,
        out_specs=(vmem,) * 4,
        scratch_shapes=[
            pltpu.VMEM((2 * RING * ROW, width + 16, width), jnp.bfloat16),
            pltpu.VMEM((tiles, 2 * width, lanes), jnp.bfloat16),
            pltpu.VMEM((window, width), jnp.bfloat16),
            [pltpu.VMEM((window, lanes), jnp.bfloat16)] * 2,
            pltpu.VMEM((2, 2, lanes, width), jnp.bfloat16),
            sem((2 * ROW - 1,)), sem((2 * ROW - 1,)), sem((2, 2)), sem((2, 2)), sem((2, 2)), sem((2, 2)),
            sem((ROW,)), sem((ROW,)),
            sem((half_ring, ROW)), sem((half_ring, ROW)), sem((half_ring, ROW)), sem((half_ring, ROW)),
            sem((RING, ROW)), sem((RING, ROW)), sem((2,)),
        ],
        compiler_params=pltpu.CompilerParams(
            collective_id=0, has_side_effects=True, vmem_limit_bytes=32 * 1024 * 1024),
        cost_estimate=pl.CostEstimate(flops=10**10, bytes_accessed=20_000_000, transcendentals=0),
    )(places, q, kv)


def finish_kernel(place_ref, order, q_all, kv_all, acc, top, o_ref, lse_ref, again_acc, again_top):
    x, z, _, _ = place()
    half = x // 2
    tiles, deep, lanes = acc.shape
    piece, width = kv_all.shape[-2:]
    block = 2 * piece
    rate = math.log2(math.e) / math.sqrt(width)
    q_row = lax.broadcasted_iota(jnp.int32, (1, lanes), 1) % block

    def stored(zc, core, at, b):
        return order[((zc // 2 * 2 + core) * RING + at * 2 + zc % 2) * EACH + b]

    def put(t, weight, sums, reference):
        some = weight > 0
        weight = jnp.where(some, weight, 1.0)
        o_ref[t] = (sums * (1.0 / weight)).T.astype(jnp.bfloat16)
        lse_ref[t] = jnp.where(some, reference + jnp.log2(weight), -1e30)

    worst = jnp.zeros((1, lanes), jnp.float32)
    for t in range(tiles):
        weight = acc[t, width:width + 1, :]
        own = (t // EACH % 2 * ROW + t // (2 * EACH)) * EACH + t % EACH
        no_key = (place_ref[z, own:own + 1, :] == 0) & (q_row < half * piece)
        fits = ((weight > 2.0**-60) & (weight < 2.0**80)) | no_key
        worst = jnp.maximum(worst, jnp.where(fits, 0.0, 1.0))
        put(t, weight, acc[t, :width, :], top[t] * rate)

    def redo(t, carry):
        at_q, core_q, b_q = t // (2 * EACH), t // EACH % 2, t % EACH
        pos = stored(z, core_q, at_q, b_q)
        q = q_all[at_q, core_q, b_q].T
        again_acc[...] = jnp.zeros_like(again_acc)
        again_top[0:1, :] = jnp.full((1, lanes), -1e30, jnp.float32)
        again_top[1:2, :] = jnp.zeros((1, lanes), jnp.float32)

        def one(g, carry):
            core, zc, at = g // (RING * ROW), g // ROW % RING, g % ROW
            for b in range(EACH):
                kp = stored(zc, core, at, b)
                k_at = lax.broadcasted_iota(jnp.int32, (piece, lanes), 0) + half * piece + kp * block
                s = jnp.dot(kv_all[core, zc, at, 0, b], q, preferred_element_type=jnp.float32) * rate
                s = jnp.where(k_at <= pos * block + q_row, s, -2e30)
                old = again_top[0:1, :]
                new = jnp.maximum(old, jnp.max(s, axis=0, keepdims=True))
                p = jnp.exp2(s - new)
                fade = jnp.exp2(old - new)
                again_top[0:1, :] = new
                again_top[1:2, :] = again_top[1:2, :] * fade + jnp.sum(p, axis=0, keepdims=True)
                v = kv_all[core, zc, at, 1, b].T
                again_acc[...] = again_acc[...] * fade + jnp.dot(
                    v, p.astype(jnp.bfloat16), preferred_element_type=jnp.float32)
            return carry

        lax.fori_loop(0, 2 * RING * ROW, one, 0)
        put(t, again_top[1:2, :], again_acc[...], again_top[0:1, :])
        return carry

    @pl.when(jnp.max(worst) > 0)
    def _():
        lax.fori_loop(0, tiles, redo, 0)


def finish(places, order, q_all, kv_all, acc, top):
    smem = pl.BlockSpec(memory_space=pltpu.SMEM)
    vmem = pl.BlockSpec(memory_space=pltpu.VMEM)
    tiles, deep, lanes = acc.shape
    width = deep - 16
    return pl.pallas_call(
        finish_kernel,
        out_shape=(jax.ShapeDtypeStruct((tiles, lanes, width), jnp.bfloat16),
                   jax.ShapeDtypeStruct((tiles, 1, lanes), jnp.float32)),
        in_specs=[vmem, smem, vmem, vmem, vmem, vmem],
        out_specs=(vmem, vmem),
        scratch_shapes=[pltpu.VMEM((width, lanes), jnp.float32), pltpu.VMEM((8, lanes), jnp.float32)],
        compiler_params=pltpu.CompilerParams(vmem_limit_bytes=20 * 1024 * 1024),
    )(places, order, q_all, kv_all, acc, top)


def return_kernel(o_ref, lse_ref, o_all, lse_all, relay, o_send, o_recv, l_send, l_recv,
                  far_send, far_recv, on_send, on_recv, own_sem):
    x, z, c, y = place()
    steps, mates = row_mates(x, z, c, y)
    mate = dict(zip(steps, mates))
    greet(mates)
    keep = [pltpu.make_async_copy(o_ref.at[x, c], o_all.at[x, c], own_sem.at[0]),
            pltpu.make_async_copy(lse_ref.at[x, c], lse_all.at[x, c], own_sem.at[1])]
    copies, far = [], []
    for side, dx in ((0, 1), (1, 3)):
        for dc in range(2):
            far.append(remote(o_ref.at[(x + 2) % ROW, (c + dc) % 2, side], relay.at[side, dc],
                              far_send.at[side, dc], far_recv.at[side, dc], mate[dx, 0]))
            far[-1].start()
    for n, (dx, dc) in enumerate(steps):
        to_x, to_c = (x + dx) % ROW, (c + dc) % 2
        copies.append(remote(lse_ref.at[to_x, to_c], lse_all.at[x, c], l_send.at[n], l_recv.at[n], mates[n]))
        copies[-1].start()
        if dx != 2:
            copies.append(remote(o_ref.at[to_x, to_c], o_all.at[x, c], o_send.at[n], o_recv.at[n], mates[n]))
            copies[-1].start()
    for copy in keep:
        copy.start()
    for k, (side, dx) in enumerate(((0, 1), (1, 3))):
        for dc in range(2):
            far[2 * k + dc].wait()
            copies.append(remote(relay.at[side, dc], o_all.at[(x + ROW - dx) % ROW, c, side],
                                 on_send.at[side, dc], on_recv.at[side, dc], mate[dx, dc]))
            copies[-1].start()
    for copy in [*keep, *copies]:
        copy.wait()


def send_back(o, lse):
    sem = pltpu.SemaphoreType.DMA
    vmem = pl.BlockSpec(memory_space=pltpu.VMEM)
    n = 2 * ROW - 1
    return pl.pallas_call(
        return_kernel,
        out_shape=(jax.ShapeDtypeStruct(o.shape, o.dtype), jax.ShapeDtypeStruct(lse.shape, lse.dtype)),
        in_specs=[vmem, vmem],
        out_specs=(vmem, vmem),
        scratch_shapes=[pltpu.VMEM((2, 2, *o.shape[-2:]), o.dtype),
                        sem((n,)), sem((n,)), sem((n,)), sem((n,)),
                        sem((2, 2)), sem((2, 2)), sem((2, 2)), sem((2, 2)), sem((2,))],
        compiler_params=pltpu.CompilerParams(
            collective_id=1, has_side_effects=True, vmem_limit_bytes=32 * 1024 * 1024),
        cost_estimate=pl.CostEstimate(flops=0, bytes_accessed=20_000_000, transcendentals=0),
    )(o, lse)


def body(stored_query_rows, stored_key_rows, stored_value_rows, span_order):
    rows, heads, width = stored_query_rows.shape
    span = rows // EACH
    q = stored_query_rows.reshape(EACH, span, 2, 2, 2, width).transpose(2, 3, 0, 4, 1, 5)
    q = q.reshape(2, 2, EACH, 2 * span, width)
    kv = jnp.stack([stored_key_rows, stored_value_rows])
    kv = kv.reshape(2, EACH, 2, span // 2, 2, width).transpose(4, 2, 0, 1, 3, 5)
    kv = kv.reshape(4, 2, EACH, span // 2, width)
    places = span_order.astype(jnp.float32).reshape(RING // 2, 2, ROW, 2, EACH).transpose(0, 3, 1, 2, 4)
    places = jnp.broadcast_to(places.reshape(RING, 2 * ROW * EACH, 1), (RING, 2 * ROW * EACH, 2 * span))
    o, lse = finish(places, span_order, *attend(places, q, kv))

    o, lse = send_back(o.reshape(ROW, 2, EACH, 2 * span, width), lse.reshape(ROW, 2, EACH, 1, 2 * span))
    o = o.reshape(2, 2, 2, EACH, 2, span, width)
    lse = lse.reshape(2, 2, 2, EACH, 2, span)
    top = jnp.max(lse, axis=0)
    weights = jnp.exp2(lse - top)
    share = weights / jnp.sum(weights, axis=0)
    result = jnp.sum(o.astype(jnp.float32) * share[..., None], axis=0).astype(jnp.bfloat16)
    return result.transpose(2, 4, 0, 1, 3, 5).reshape(rows, heads, width)


def solution(mesh):
    placed = (
        P(("outer", "inner"), "head", None),
        P(("outer", "inner"), "head", None),
        P(("outer", "inner"), "head", None),
        P(),
    )
    return jax.shard_map(
        body,
        mesh=mesh,
        in_specs=placed,
        out_specs=P(("outer", "inner"), "head", None),
        check_vma=False,
    )
```

time: 115 us -> 87.7 us (0.76)
  the two profiles are of different devices: /device:TPU:97 before, /device:TPU:1 now
where the time goes in v3:
time: 87.7 us; the launch traced here: 87.5 us
  Pallas kernels  81.3 us (93%)
  local copies, waits for them, and re-layouts  4.52 us (5%)
  other arithmetic  1.57 us (2%)
    pallas_call x1, Pallas kernels, attend(): pl.pallas_call(attend_kernel, out_shape=(jax.ShapeDtypeStruct((ROW, 2, *q...  64.6 us
    pallas_call x1, Pallas kernels, send_back(): pl.pallas_call(return_kernel, out_shape=(jax.ShapeDtypeStruct(o.shape, o....  15.7 us
    another operation x2, local copies, waits for them, and re-layouts, body(): kv = jnp.stack([stored_key_rows, stored_value_rows])  1.85 us

profile of v3, /device:TPU:1, one launch (start us, length us, event | category | flops | bytes accessed | tf_op | source)
XLA Modules:
  0.0 87.5 jit_solution(2477096002295172688)
XLA Ops:
  0.0 0.7 convert_element_type.16
  0.7 0.2 reshape.48
  0.8 0.1 broadcast_in_dim.4
  0.9 0.1 broadcast_in_dim.5.place_ref
  1.0 0.9 %copy.19 = bf16[1,2,2,64,2,128]{5,3,1,0,2,4:T(8,128)(2,1)S(1)} copy(bf16[1,2,2,64,2,128]{5,4,3,2,1,0:T(2,128)(2,1)} %bitcast.30) | data formatting | bytes 262144 | tf_op jit(solution)/shard_map/stack | solution.py:434
  1.9 0.9 %copy.20 = bf16[1,2,2,64,2,128]{5,3,1,0,2,4:T(8,128)(2,1)S(1)} copy(bf16[1,2,2,64,2,128]{5,4,3,2,1,0:T(2,128)(2,1)} %bitcast.31) | data formatting | bytes 262144 | tf_op jit(solution)/shard_map/stack | solution.py:434
  2.9 1.1 %copy.18 = bf16[2,128,2,2,2,128]{5,1,4,0,3,2:T(8,128)(2,1)S(1)} copy(bf16[2,128,2,2,2,128]{5,4,3,2,1,0:T(2,128)(2,1)} %bitcast.29) | data formatting | bytes 1048576 | tf_op jit(solution)/shard_map/reshape | solution.py:432
  4.1 0.0 copy-start
  4.1 64.6 %shard_map.46 = (bf16[4,2,2,256,128]{4,3,2,1,0:T(8,128)(2,1)S(1)}, bf16[2,8,4,2,2,64,128]{6,5,4,3,2,1,0:T(8,128)(2,1)S(1)}, f32[16,144,256]{2,1,0:T(8,128)S(1)}, f32[16,1,256]{2,1,0:T(1,128)S(1)}) custom-call(f32[8,16,256]{2,1,0:T(8,128)S(1)} %broadcast_in_dim.5.place_ref, bf16[2,2,2,256,128]{4,3,2,1,0:T(8,128)(2,1)S(1)} %bitcast.21, ...), custom_call_target="tpu_custom_call" | custom-call | flops 10000000000 | bytes 20000000 | tf_op jit(solution)/shard_map/pallas_call | solution.py:275
  68.7 0.0 copy-done
  68.7 1.0 %shard_map.47 = (bf16[16,256,128]{2,1,0:T(8,128)(2,1)S(1)}, f32[16,1,256]{2,1,0:T(1,128)S(1)}) custom-call(f32[8,16,256]{2,1,0:T(8,128)S(1)} %broadcast_in_dim.5.place_ref, s32[128]{0:T(128)S(1)} %copy-done, bf16[4,2,2,256,128]{4,3,2,1,0:T(8,128)(2,1)S(1)} %get-tuple-element.13.q_all, bf16[2,8,4,2,2,64,128]{6,5,4,3,2,1,0:T(8,128)(2,1)S(1)} %get-tuple-element.14.kv_all, ...), custom_call_target="tpu_custom_call" | custom-call | tf_op jit(solution)/shard_map/pallas_call | solution.py:367
  69.7 15.7 %shard_map.48 = (bf16[4,2,2,256,128]{4,3,2,1,0:T(8,128)(2,1)S(1)}, f32[4,2,2,1,256]{4,3,2,1,0:T(1,128)S(1)}) custom-call(bf16[4,2,2,256,128]{4,3,2,1,0:T(8,128)(2,1)S(1)} %bitcast.20, f32[4,2,2,1,256]{4,3,2,1,0:T(1,128)S(1)} %bitcast.26), custom_call_target="tpu_custom_call" | custom-call | bytes 20000000 | tf_op jit(solution)/shard_map/pallas_call | solution.py:415
  85.5 0.8 fusion
  86.4 1.1 %copy.22 = bf16[256,8,128]{2,1,0:T(8,128)(2,1)} copy(bf16[256,8,128]{2,0,1:T(8,128)(2,1)S(1)} %bitcast.28) | data formatting | bytes 1048576 | tf_op jit(solution)/shard_map/reshape | solution.py:448
  (6 shorter events, 0.2 us)
Async XLA Ops:
  4.1 64.7 %copy-start = (s32[128]{0:T(128)S(1)}, s32[128]{0:T(128)}, u32[]{:S(2)}) copy-start(s32[128]{0:T(128)} %order.1) | copy-start | bytes 1540

commit v4 on v3

--- a/solution.py
+++ b/solution.py
@@ -40,7 +40,7 @@
         src_ref=src, dst_ref=dst, send_sem=send, recv_sem=recv, device_id=to, device_id_type=MESH)
 
 
-def attend_kernel(place_ref, q_ref, kv_ref, q_all, kv_all, acc, top,
+def attend_kernel(place_ref, q_ref, kv_ref, q_all, kv_all, acc, total, top,
                   v_turned, q_turned, marks, p_bufs, relay,
                   q_send, q_recv, far_send, far_recv, on_send, on_recv, x_send, x_recv,
                   up_send, up_recv, down_send, down_recv, core_send, core_recv, own_sem):
@@ -90,20 +90,19 @@
     keep_q = pltpu.make_async_copy(q_ref.at[x % 2, c], q_all.at[x, c], own_sem.at[1])
     keep_kv.start()
     keep_q.start()
+    for n, (dx, dc) in enumerate(steps):
+        if dx != 2:
+            remote(q_ref.at[(x + dx) % 2, (c + dc) % 2], q_all.at[x, c], q_send.at[n], q_recv.at[n],
+                   mates[n]).start()
     for side, dx in ((0, 1), (1, 3)):
         for dc in range(2):
             remote(q_ref.at[x % 2, (c + dc) % 2, side], relay.at[side, dc], far_send.at[side, dc],
                    far_recv.at[side, dc], mate[dx, 0]).start()
-    for n, (dx, dc) in enumerate(steps):
-        if dx != 2:
-            remote(q_ref.at[(x + dx) % 2, (c + dc) % 2], q_all.at[x, c], q_send.at[n], q_recv.at[n],
-                   mates[n]).start()
 
     k_row = lax.broadcasted_iota(jnp.int32, (window, width), 0)
     column = lax.broadcasted_iota(jnp.int32, (window, width), 1)
     marks[...] = jnp.where((column == k_row // piece) | (column == tiles), 1.0, 0.0).astype(marks.dtype)
     q_turned[:, width + tiles:, :] = jnp.zeros((tiles, width - tiles, lanes), q_turned.dtype)
-    v_turned[:, width:, :] = jnp.ones((v_turned.shape[0], v_turned.shape[1] - width, width), v_turned.dtype)
 
     for j in (1, 3, 2):
         slot = slot_of(0, j)
@@ -111,13 +110,15 @@
         pass_up(0, j, slot)
         pass_down(0, j, slot)
         to_partner(0, j, slot)
-    for side, dx in ((0, 1), (1, 3)):
-        for dc in range(2):
-            arrived(relay.at[side, dc], far_recv.at[side, dc])
-            remote(relay.at[side, dc], q_all.at[(x + ROW - dx) % ROW, c, side], on_send.at[side, dc],
-                   on_recv.at[side, dc], mate[dx, dc]).start()
     keep_kv.wait()
     keep_q.wait()
+
+    def forward():
+        for side, dx in ((0, 1), (1, 3)):
+            for dc in range(2):
+                arrived(relay.at[side, dc], far_recv.at[side, dc])
+                remote(relay.at[side, dc], q_all.at[(x + ROW - dx) % ROW, c, side], on_send.at[side, dc],
+                       on_recv.at[side, dc], mate[dx, dc]).start()
 
     def ready(zc):
         r = (zc - z + RING) % RING
@@ -126,7 +127,7 @@
         for core in range(2):
             for at in range(ROW):
                 v = kv_all[core, zc, at, 1].reshape(EACH * piece, width)
-                v_turned[(core * RING + zc) * ROW + at, :width, :] = v.T
+                v_turned[(core * RING + zc) * ROW + at] = v.T
 
     ready(z)
 
@@ -143,23 +144,24 @@
             top[t] = ref
             first = lax.broadcasted_iota(jnp.int32, (tiles, lanes), 0) == 0
             q_turned[t, width + tiles:width + 2 * tiles, :] = jnp.where(first, -ref, 0.0).astype(q_turned.dtype)
-            p = jnp.where(own_allowed, jnp.exp2((s - ref) * rate), 0.0).astype(jnp.bfloat16)
+            p = jnp.where(own_allowed, jnp.exp2((s - ref) * rate), 0.0)
+            total[t] = jnp.sum(p.reshape(piece // 8, 8, lanes), axis=0)
             v = v_turned[(core * RING + z) * ROW + at]
-            acc[t] = jnp.dot(v[:, b * piece:(b + 1) * piece], p, preferred_element_type=jnp.float32)
+            acc[t] = jnp.dot(v[:, b * piece:(b + 1) * piece], p.astype(jnp.bfloat16), preferred_element_type=jnp.float32)
 
     take(x, c)
     arrived(q_all.at[x, 1 - c], q_recv.at[steps.index((0, 1))])
     take(x, 1 - c)
-    for dx in (1, 3):
-        for dc in range(2):
-            core = (c + dc) % 2
-            arrived(q_all.at[(x + ROW - dx) % ROW, core], q_recv.at[steps.index((dx, dc))])
-            take((x + ROW - dx) % ROW, core)
-    for dc in range(2):
-        core = (c + dc) % 2
-        for side in range(2):
-            arrived(q_all.at[(x + 2) % ROW, core, side], on_recv.at[side, dc])
-        take((x + 2) % ROW, core)
+
+    def await_queries(dx):
+        for core in range(2):
+            if dx == 2:
+                for side in range(2):
+                    dc = (core + c) % 2
+                    arrived(q_all.at[(x + 2) % ROW, core, side], on_recv.at[side, dc])
+            else:
+                dc = (core + c) % 2
+                arrived(q_all.at[(x + ROW - dx) % ROW, core], q_recv.at[steps.index((dx, 0)) + dc])
 
     def row_at(n):
         off = jnp.where(n % 2 == 1, -((n + 1) // 2), n // 2)
@@ -172,7 +174,9 @@
         k = [kv_all[core, zc, at, 0].reshape(EACH * piece, width) for core in range(2) for at in range(ROW)]
         keys = jnp.concatenate([jnp.concatenate(k, axis=0), marks[...]], axis=1)
         s = jnp.dot(keys, q_turned[t], preferred_element_type=jnp.float32)
-        p_bufs[buf][...] = jnp.exp2(s * rate).astype(jnp.bfloat16)
+        p = jnp.exp2(s * rate)
+        total[t] += jnp.sum(p.reshape(window // 8, 8, lanes), axis=0)
+        p_bufs[buf][...] = p.astype(jnp.bfloat16)
 
     def absorb(t, zc, buf):
         v = [v_turned[(core * RING + zc) * ROW + at] for core in range(2) for at in range(ROW)]
@@ -210,40 +214,70 @@
             arrived(slot, up_recv.at[3, j] if j < 2 else down_recv.at[3, j])
             to_partner(RING // 2, j, slot)
 
-    per_turn = 4
-    turns = tiles // per_turn
+    for j in (0, 1, 3, 2):
+        relay_on(0, j)
+        relay_on(1, j)
+
+    per_turn = 2 * EACH
+    turns = ROW * RING
+    early = 3
+
+    def plan(m):
+        first = m < early * ROW
+        n = jnp.where(first, m % early, m // ROW)
+        g = jnp.where(first, m // early, m % ROW)
+        chip = (x + jnp.where(g == 1, 3, jnp.where(g == 2, 1, jnp.where(g == 3, 2, 0)))) % ROW
+        return chip, chip * per_turn, row_at(n)[1]
 
     def turn(m, carry):
-        n, i = m // turns, m % turns
-        _, zc = row_at(n)
-        _, ahead = row_at(jnp.minimum(n + 1, RING - 1))
-
-        @pl.when(i == 0)
+        _, base, zc = plan(m)
+        chip, next_base, next_zc = plan(m + 1)
+        n, i = m // ROW, m % ROW
+
+        @pl.when((m < early - 1) | ((m >= 2 * ROW) & (i == ROW - 1) & (m < turns - 1)))
+        def _():
+            ready(next_zc)
+
+        for g, dx in ((1, 1), (2, 3), (3, 2)):
+            @pl.when(m == early * g - 1)
+            def _(dx=dx):
+                await_queries(dx)
+
+        @pl.when(m == early + 1)
+        def _():
+            forward()
+
+        @pl.when((m == early - 1) | (m == 2 * early - 1) | (m == 3 * early - 1))
+        def _():
+            take(chip, 0)
+            take(chip, 1)
+
+        @pl.when((m >= 2 * ROW) & (i == 0))
         def _():
             relay_on(n, 0)
             relay_on(n, 1)
 
-        @pl.when(i == 1)
+        @pl.when((m >= 2 * ROW) & (i == 1))
         def _():
             relay_on(n, 3)
 
-        @pl.when(i == 2)
+        @pl.when((m >= 2 * ROW) & (i == 2))
         def _():
             relay_on(n, 2)
 
-        @pl.when((i == turns - 1) & (n < RING - 1))
-        def _():
-            ready(ahead)
-
         for u in range(per_turn):
-            t = i * per_turn + u
-            wrap = t == tiles - 1
-            weigh(jnp.where(wrap, 0, t + 1), jnp.where(wrap, ahead, zc), 1 - u % 2)
-            absorb(t, zc, u % 2)
+            done = u == per_turn - 1
+            weigh(next_base if done else base + u + 1, next_zc if done else zc, 1 - u % 2)
+            absorb(base + u, zc, u % 2)
         return carry
 
-    weigh(0, z, 0)
-    lax.fori_loop(0, RING * turns, turn, 0)
+    weigh(x * per_turn, z, 0)
+    lax.fori_loop(0, turns - 1, turn, 0)
+    _, last_base, last_zc = plan(turns - 1)
+    for u in range(per_turn):
+        if u < per_turn - 1:
+            weigh(last_base + u + 1, last_zc, 1 - u % 2)
+        absorb(last_base + u, last_zc, u % 2)
 
     for j in range(ROW):
         for t in range(RING // 2):
@@ -276,12 +310,13 @@
         attend_kernel,
         out_shape=(jax.ShapeDtypeStruct((ROW, 2, *q.shape[2:]), q.dtype),
                    jax.ShapeDtypeStruct((2, RING, ROW, *kv.shape[1:]), kv.dtype),
-                   jax.ShapeDtypeStruct((tiles, width + 16, lanes), jnp.float32),
+                   jax.ShapeDtypeStruct((tiles, width, lanes), jnp.float32),
+                   jax.ShapeDtypeStruct((tiles, 8, lanes), jnp.float32),
                    jax.ShapeDtypeStruct((tiles, 1, lanes), jnp.float32)),
         in_specs=[vmem] * 3,
-        out_specs=(vmem,) * 4,
+        out_specs=(vmem,) * 5,
         scratch_shapes=[
-            pltpu.VMEM((2 * RING * ROW, width + 16, width), jnp.bfloat16),
+            pltpu.VMEM((2 * RING * ROW, width, width), jnp.bfloat16),
             pltpu.VMEM((tiles, 2 * width, lanes), jnp.bfloat16),
             pltpu.VMEM((window, width), jnp.bfloat16),
             [pltpu.VMEM((window, lanes), jnp.bfloat16)] * 2,
@@ -297,10 +332,10 @@
     )(places, q, kv)
 
 
-def finish_kernel(place_ref, order, q_all, kv_all, acc, top, o_ref, lse_ref, again_acc, again_top):
+def finish_kernel(place_ref, order, q_all, kv_all, acc, total, top, o_ref, lse_ref, again_acc, again_top):
     x, z, _, _ = place()
     half = x // 2
-    tiles, deep, lanes = acc.shape
+    tiles, _, lanes = acc.shape
     piece, width = kv_all.shape[-2:]
     block = 2 * piece
     rate = math.log2(math.e) / math.sqrt(width)
@@ -317,12 +352,12 @@
 
     worst = jnp.zeros((1, lanes), jnp.float32)
     for t in range(tiles):
-        weight = acc[t, width:width + 1, :]
+        weight = jnp.sum(total[t], axis=0, keepdims=True)
         own = (t // EACH % 2 * ROW + t // (2 * EACH)) * EACH + t % EACH
         no_key = (place_ref[z, own:own + 1, :] == 0) & (q_row < half * piece)
         fits = ((weight > 2.0**-60) & (weight < 2.0**80)) | no_key
         worst = jnp.maximum(worst, jnp.where(fits, 0.0, 1.0))
-        put(t, weight, acc[t, :width, :], top[t] * rate)
+        put(t, weight, acc[t], top[t] * rate)
 
     def redo(t, carry):
         at_q, core_q, b_q = t // (2 * EACH), t // EACH % 2, t % EACH
@@ -359,20 +394,19 @@
         lax.fori_loop(0, tiles, redo, 0)
 
 
-def finish(places, order, q_all, kv_all, acc, top):
+def finish(places, order, q_all, kv_all, acc, total, top):
     smem = pl.BlockSpec(memory_space=pltpu.SMEM)
     vmem = pl.BlockSpec(memory_space=pltpu.VMEM)
-    tiles, deep, lanes = acc.shape
-    width = deep - 16
+    tiles, width, lanes = acc.shape
     return pl.pallas_call(
         finish_kernel,
         out_shape=(jax.ShapeDtypeStruct((tiles, lanes, width), jnp.bfloat16),
                    jax.ShapeDtypeStruct((tiles, 1, lanes), jnp.float32)),
-        in_specs=[vmem, smem, vmem, vmem, vmem, vmem],
+        in_specs=[vmem, smem, vmem, vmem, vmem, vmem, vmem],
         out_specs=(vmem, vmem),
         scratch_shapes=[pltpu.VMEM((width, lanes), jnp.float32), pltpu.VMEM((8, lanes), jnp.float32)],
         compiler_params=pltpu.CompilerParams(vmem_limit_bytes=20 * 1024 * 1024),
-    )(places, order, q_all, kv_all, acc, top)
+    )(places, order, q_all, kv_all, acc, total, top)
 
 
 def return_kernel(o_ref, lse_ref, o_all, lse_all, relay, o_send, o_recv, l_send, l_recv,

time: 87.7 us -> 89.2 us (1.017)
  Pallas kernels: 81.3 us -> 82.8 us
    pallas_call x1, Pallas kernels: 64.6 us -> 65.8 us  [attend(): pl.pallas_call(attend_kernel, out_shape=(jax.ShapeDtypeStruct((ROW, 2, *q...]
where the time goes in v4:
time: 89.2 us; the launch traced here: 89 us
  Pallas kernels  82.8 us (93%)
  local copies, waits for them, and re-layouts  4.52 us (5%)
  other arithmetic  1.57 us (2%)
    pallas_call x1, Pallas kernels, attend(): pl.pallas_call(attend_kernel, out_shape=(jax.ShapeDtypeStruct((ROW, 2, *q...  65.8 us
    pallas_call x1, Pallas kernels, send_back(): pl.pallas_call(return_kernel, out_shape=(jax.ShapeDtypeStruct(o.shape, o....  16 us
    another operation x2, local copies, waits for them, and re-layouts, body(): kv = jnp.stack([stored_key_rows, stored_value_rows])  1.85 us

profile of v4, /device:TPU:1, one launch (start us, length us, event | category | flops | bytes accessed | tf_op | source)
XLA Modules:
  0.0 89.0 jit_solution(13571746699733858030)
XLA Ops:
  0.0 0.7 convert_element_type.16
  0.7 0.2 reshape.48
  0.8 0.1 broadcast_in_dim.4
  0.9 0.1 broadcast_in_dim.5.place_ref
  1.0 0.9 %copy.19 = bf16[1,2,2,64,2,128]{5,3,1,0,2,4:T(8,128)(2,1)S(1)} copy(bf16[1,2,2,64,2,128]{5,4,3,2,1,0:T(2,128)(2,1)} %bitcast.30) | data formatting | bytes 262144 | tf_op jit(solution)/shard_map/stack | solution.py:468
  1.9 0.9 %copy.20 = bf16[1,2,2,64,2,128]{5,3,1,0,2,4:T(8,128)(2,1)S(1)} copy(bf16[1,2,2,64,2,128]{5,4,3,2,1,0:T(2,128)(2,1)} %bitcast.31) | data formatting | bytes 262144 | tf_op jit(solution)/shard_map/stack | solution.py:468
  2.9 1.1 %copy.18 = bf16[2,128,2,2,2,128]{5,1,4,0,3,2:T(8,128)(2,1)S(1)} copy(bf16[2,128,2,2,2,128]{5,4,3,2,1,0:T(2,128)(2,1)} %bitcast.29) | data formatting | bytes 1048576 | tf_op jit(solution)/shard_map/reshape | solution.py:466
  4.1 0.0 copy-start
  4.1 65.8 %shard_map.46 = (bf16[4,2,2,256,128]{4,3,2,1,0:T(8,128)(2,1)S(1)}, bf16[2,8,4,2,2,64,128]{6,5,4,3,2,1,0:T(8,128)(2,1)S(1)}, f32[16,128,256]{2,1,0:T(8,128)S(1)},...) custom-call(f32[8,16,256]{2,1,0:T(8,128)S(1)} %broadcast_in_dim.5.place_ref, bf16[2,2,2,256,128]{4,3,2,1,0:T(8,128)(2,1)S(1)} %bitcast.21, ...), custom_call_target="tpu_custom_call" | custom-call | flops 10000000000 | bytes 20000000 | tf_op jit(solution)/shard_map/pallas_call | solution.py:309
  69.9 0.0 copy-done
  69.9 1.0 %shard_map.47 = (bf16[16,256,128]{2,1,0:T(8,128)(2,1)S(1)}, f32[16,1,256]{2,1,0:T(1,128)S(1)}) custom-call(f32[8,16,256]{2,1,0:T(8,128)S(1)} %broadcast_in_dim.5.place_ref, s32[128]{0:T(128)S(1)} %copy-done, bf16[4,2,2,256,128]{4,3,2,1,0:T(8,128)(2,1)S(1)} %get-tuple-element.14.q_all, bf16[2,8,4,2,2,64,128]{6,5,4,3,2,1,0:T(8,128)(2,1)S(1)} %get-tuple-element.15.kv_all, ...), custom_call_target="tpu_custom_call" | custom-call | tf_op jit(solution)/shard_map/pallas_call | solution.py:401
  71.0 16.0 %shard_map.48 = (bf16[4,2,2,256,128]{4,3,2,1,0:T(8,128)(2,1)S(1)}, f32[4,2,2,1,256]{4,3,2,1,0:T(1,128)S(1)}) custom-call(bf16[4,2,2,256,128]{4,3,2,1,0:T(8,128)(2,1)S(1)} %bitcast.20, f32[4,2,2,1,256]{4,3,2,1,0:T(1,128)S(1)} %bitcast.26), custom_call_target="tpu_custom_call" | custom-call | bytes 20000000 | tf_op jit(solution)/shard_map/pallas_call | solution.py:449
  87.0 0.8 fusion
  87.9 1.1 %copy.22 = bf16[256,8,128]{2,1,0:T(8,128)(2,1)} copy(bf16[256,8,128]{2,0,1:T(8,128)(2,1)S(1)} %bitcast.28) | data formatting | bytes 1048576 | tf_op jit(solution)/shard_map/reshape | solution.py:482
  (6 shorter events, 0.2 us)
Async XLA Ops:
  4.1 65.9 %copy-start = (s32[128]{0:T(128)S(1)}, s32[128]{0:T(128)}, u32[]{:S(2)}) copy-start(s32[128]{0:T(128)} %order.1) | copy-start | bytes 1540

commit v5 on v4

--- a/solution.py
+++ b/solution.py
@@ -10,6 +10,7 @@
 ROW = 4
 RING = 8
 EACH = 2
+NEAR = 3
 MESH = pl.DeviceIdType.MESH
 NEVER = 2.0**20
 
@@ -40,8 +41,8 @@
         src_ref=src, dst_ref=dst, send_sem=send, recv_sem=recv, device_id=to, device_id_type=MESH)
 
 
-def attend_kernel(place_ref, q_ref, kv_ref, q_all, kv_all, acc, total, top,
-                  v_turned, q_turned, marks, p_bufs, relay,
+def attend_kernel(place_ref, q_ref, kv_ref, q_all, kv_all, acc, total, top, q_turned, marks,
+                  v_turned, p_bufs, relay,
                   q_send, q_recv, far_send, far_recv, on_send, on_recv, x_send, x_recv,
                   up_send, up_recv, down_send, down_recv, core_send, core_recv, own_sem):
     x, z, c, y = place()
@@ -182,88 +183,67 @@
         v = [v_turned[(core * RING + zc) * ROW + at] for core in range(2) for at in range(ROW)]
         acc[t] += jnp.dot(jnp.concatenate(v, axis=1), p_bufs[buf][...], preferred_element_type=jnp.float32)
 
-    def relay_on(n, j):
-        t = n // 2 + 1
-        rising = n % 2 == 0
-
-        @pl.when((n < 6) & rising)
+    def rise(t, j):
+        slot = slot_of(-t, j)
+        arrived(slot, up_recv.at[t - 1, j])
+
+        @pl.when((t < 3) | ((t == 3) & (j < 2)))
         def _():
-            slot = slot_of(-t, j)
-            arrived(slot, up_recv.at[t - 1, j])
-
-            @pl.when((t < 3) | (j < 2))
-            def _():
-                pass_up(t, j, slot)
-
-            to_partner(-t, j, slot)
-
-        @pl.when((n < 6) & jnp.logical_not(rising))
+            pass_up(t, j, slot)
+
+        to_partner(-t, j, slot)
+
+    def fall(t, j):
+        slot = slot_of(t, j)
+        arrived(slot, down_recv.at[t - 1, j])
+
+        @pl.when((t < 3) | ((t == 3) & (j >= 2)))
         def _():
-            slot = slot_of(t, j)
-            arrived(slot, down_recv.at[t - 1, j])
-
-            @pl.when((t < 3) | (j >= 2))
-            def _():
-                pass_down(t, j, slot)
-
-            to_partner(t, j, slot)
-
-        @pl.when(n == 6)
-        def _():
-            slot = slot_of(RING // 2, j)
-            arrived(slot, up_recv.at[3, j] if j < 2 else down_recv.at[3, j])
-            to_partner(RING // 2, j, slot)
+            pass_down(t, j, slot)
+
+        to_partner(t, j, slot)
 
     for j in (0, 1, 3, 2):
-        relay_on(0, j)
-        relay_on(1, j)
+        rise(1, j)
+        fall(1, j)
 
     per_turn = 2 * EACH
-    turns = ROW * RING
-    early = 3
+    turns = ROW * NEAR
 
     def plan(m):
-        first = m < early * ROW
-        n = jnp.where(first, m % early, m // ROW)
-        g = jnp.where(first, m // early, m % ROW)
+        g = m // NEAR
         chip = (x + jnp.where(g == 1, 3, jnp.where(g == 2, 1, jnp.where(g == 3, 2, 0)))) % ROW
-        return chip, chip * per_turn, row_at(n)[1]
+        return chip, chip * per_turn, row_at(m % NEAR)[1]
 
     def turn(m, carry):
         _, base, zc = plan(m)
         chip, next_base, next_zc = plan(m + 1)
-        n, i = m // ROW, m % ROW
-
-        @pl.when((m < early - 1) | ((m >= 2 * ROW) & (i == ROW - 1) & (m < turns - 1)))
+
+        @pl.when(m < NEAR - 1)
         def _():
             ready(next_zc)
 
+        @pl.when((m >= NEAR) & (m < NEAR + 2 * ROW))
+        def _():
+            event = m - NEAR
+            t, j = event // ROW + 2, event % ROW
+            j = jnp.where(j == 2, 3, jnp.where(j == 3, 2, j))
+            rise(t, j)
+            fall(t, j)
+
         for g, dx in ((1, 1), (2, 3), (3, 2)):
-            @pl.when(m == early * g - 1)
+            @pl.when(m == NEAR * g - 1)
             def _(dx=dx):
                 await_queries(dx)
 
-        @pl.when(m == early + 1)
+        @pl.when(m == NEAR + 1)
         def _():
             forward()
 
-        @pl.when((m == early - 1) | (m == 2 * early - 1) | (m == 3 * early - 1))
+        @pl.when((m == NEAR - 1) | (m == 2 * NEAR - 1) | (m == 3 * NEAR - 1))
         def _():
             take(chip, 0)
             take(chip, 1)
-
-        @pl.when((m >= 2 * ROW) & (i == 0))
-        def _():
-            relay_on(n, 0)
-            relay_on(n, 1)
-
-        @pl.when((m >= 2 * ROW) & (i == 1))
-        def _():
-            relay_on(n, 3)
-
-        @pl.when((m >= 2 * ROW) & (i == 2))
-        def _():
-            relay_on(n, 2)
 
         for u in range(per_turn):
             done = u == per_turn - 1
@@ -273,11 +253,17 @@
 
     weigh(x * per_turn, z, 0)
     lax.fori_loop(0, turns - 1, turn, 0)
+    for up_j, down_j in ((0, 3), (1, 2)):
+        rise(RING // 2, up_j)
+        fall(RING // 2, down_j)
     _, last_base, last_zc = plan(turns - 1)
     for u in range(per_turn):
         if u < per_turn - 1:
             weigh(last_base + u + 1, last_zc, 1 - u % 2)
         absorb(last_base + u, last_zc, u % 2)
+    for r in range(2, RING - 1):
+        for j in range(ROW):
+            arrived(kv_all.at[1 - c, (z + r) % RING, (x + j) % ROW], core_recv.at[r, j])
 
     for j in range(ROW):
         for t in range(RING // 2):
@@ -312,13 +298,13 @@
                    jax.ShapeDtypeStruct((2, RING, ROW, *kv.shape[1:]), kv.dtype),
                    jax.ShapeDtypeStruct((tiles, width, lanes), jnp.float32),
                    jax.ShapeDtypeStruct((tiles, 8, lanes), jnp.float32),
-                   jax.ShapeDtypeStruct((tiles, 1, lanes), jnp.float32)),
+                   jax.ShapeDtypeStruct((tiles, 1, lanes), jnp.float32),
+                   jax.ShapeDtypeStruct((tiles, 2 * width, lanes), jnp.bfloat16),
+                   jax.ShapeDtypeStruct((window, width), jnp.bfloat16)),
         in_specs=[vmem] * 3,
-        out_specs=(vmem,) * 5,
+        out_specs=(vmem,) * 7,
         scratch_shapes=[
             pltpu.VMEM((2 * RING * ROW, width, width), jnp.bfloat16),
-            pltpu.VMEM((tiles, 2 * width, lanes), jnp.bfloat16),
-            pltpu.VMEM((window, width), jnp.bfloat16),
             [pltpu.VMEM((window, lanes), jnp.bfloat16)] * 2,
             pltpu.VMEM((2, 2, lanes, width), jnp.bfloat16),
             sem((2 * ROW - 1,)), sem((2 * ROW - 1,)), sem((2, 2)), sem((2, 2)), sem((2, 2)), sem((2, 2)),
@@ -332,7 +318,8 @@
     )(places, q, kv)
 
 
-def finish_kernel(place_ref, order, q_all, kv_all, acc, total, top, o_ref, lse_ref, again_acc, again_top):
+def finish_kernel(place_ref, order, rank, q_all, kv_all, acc, total, top, q_turned, marks, o_ref, lse_ref,
+                  k_sorted, v_sorted, v_turned, p_bufs, far_acc, far_total, again_acc, again_top):
     x, z, _, _ = place()
     half = x // 2
     tiles, _, lanes = acc.shape
@@ -350,14 +337,82 @@
         o_ref[t] = (sums * (1.0 / weight)).T.astype(jnp.bfloat16)
         lse_ref[t] = jnp.where(some, reference + jnp.log2(weight), -1e30)
 
+    window = marks.shape[0]
+    per_window = window // piece
+
+    def sort(i, carry):
+        n, g = i // (2 * ROW), i % (2 * ROW)
+        off = jnp.where(n % 2 == 1, (n + 3) // 2, -((n + 4) // 2))
+        zc = (z + off + RING) % RING
+        core, at_x = g // ROW, g % ROW
+        for b in range(EACH):
+            at = pl.multiple_of(rank[((zc * 2 + core) * ROW + at_x) * EACH + b] * piece, piece)
+            k_sorted[pl.ds(at, piece), :] = kv_all[core, zc, at_x, 0, b]
+            v_sorted[pl.ds(at, piece), :] = kv_all[core, zc, at_x, 1, b]
+        return carry
+
+    lax.fori_loop(0, (RING - NEAR) * 2 * ROW, sort, 0, unroll=4)
+
+    def turn(g, carry):
+        at = pl.multiple_of(g * width, width)
+        v_turned[g] = v_sorted[pl.ds(at, width), :].T
+        return carry
+
+    lax.fori_loop(0, v_turned.shape[0], turn, 0, unroll=8)
+
+    def own_row(t):
+        return (t // EACH % 2 * ROW + t // (2 * EACH)) * EACH + t % EACH
+
+    def count_of(t):
+        held = rank[z * tiles + own_row(jnp.minimum(t, tiles - 1))]
+        return jnp.where(t < tiles, held, 0)
+
+    def clear(t, items):
+        far_acc[t] = jnp.zeros(far_acc.shape[1:], jnp.float32)
+        far_total[t] = jnp.zeros(far_total.shape[1:], jnp.float32)
+        return items + jnp.maximum((count_of(t) + per_window - 1) // per_window, 1)
+
+    items = lax.fori_loop(0, tiles, clear, 0)
+    block_row = lax.broadcasted_iota(jnp.int32, (tiles, lanes), 0)
+
+    def weigh(t, w, buf):
+        count, t = count_of(t), jnp.minimum(t, tiles - 1)
+        at = pl.multiple_of(w * window, window)
+        mask = jnp.where(block_row < count - w * per_window, 0.0, -NEVER).astype(q_turned.dtype)
+        right = jnp.concatenate([q_turned[t, :width, :], mask, q_turned[t, width + tiles:, :]], axis=0)
+        keys = jnp.concatenate([k_sorted[pl.ds(at, window), :], marks[...]], axis=1)
+        p = jnp.exp2(jnp.dot(keys, right, preferred_element_type=jnp.float32) * rate)
+        far_total[t] += jnp.sum(p.reshape(window // 8, 8, lanes), axis=0)
+        p_bufs[buf][...] = p.astype(jnp.bfloat16)
+
+    def absorb(t, w, buf):
+        t = jnp.minimum(t, tiles - 1)
+        v = [v_turned[w * (window // width) + i] for i in range(window // width)]
+        far_acc[t] += jnp.dot(jnp.concatenate(v, axis=1), p_bufs[buf][...], preferred_element_type=jnp.float32)
+
+    unroll = 4
+
+    def step(i, at):
+        t, w = at
+        for u in range(unroll):
+            last = (w + 1) * per_window >= count_of(t)
+            next_t, next_w = jnp.where(last, t + 1, t), jnp.where(last, 0, w + 1)
+            weigh(next_t, next_w, 1 - u % 2)
+            absorb(t, w, u % 2)
+            t, w = next_t, next_w
+        return t, w
+
+    weigh(jnp.int32(0), jnp.int32(0), 0)
+    lax.fori_loop(0, (items + unroll - 1) // unroll, step, (jnp.int32(0), jnp.int32(0)))
+
     worst = jnp.zeros((1, lanes), jnp.float32)
     for t in range(tiles):
-        weight = jnp.sum(total[t], axis=0, keepdims=True)
-        own = (t // EACH % 2 * ROW + t // (2 * EACH)) * EACH + t % EACH
+        weight = jnp.sum(total[t] + far_total[t], axis=0, keepdims=True)
+        own = own_row(t)
         no_key = (place_ref[z, own:own + 1, :] == 0) & (q_row < half * piece)
         fits = ((weight > 2.0**-60) & (weight < 2.0**80)) | no_key
         worst = jnp.maximum(worst, jnp.where(fits, 0.0, 1.0))
-        put(t, weight, acc[t], top[t] * rate)
+        put(t, weight, acc[t] + far_acc[t], top[t] * rate)
 
     def redo(t, carry):
         at_q, core_q, b_q = t // (2 * EACH), t // EACH % 2, t % EACH
@@ -394,19 +449,29 @@
         lax.fori_loop(0, tiles, redo, 0)
 
 
-def finish(places, order, q_all, kv_all, acc, total, top):
+def finish(places, order, rank, q_all, kv_all, acc, total, top, q_turned, marks):
     smem = pl.BlockSpec(memory_space=pltpu.SMEM)
     vmem = pl.BlockSpec(memory_space=pltpu.VMEM)
     tiles, width, lanes = acc.shape
+    far = (RING - NEAR) * 2 * ROW * EACH * kv_all.shape[-2]
     return pl.pallas_call(
         finish_kernel,
         out_shape=(jax.ShapeDtypeStruct((tiles, lanes, width), jnp.bfloat16),
                    jax.ShapeDtypeStruct((tiles, 1, lanes), jnp.float32)),
-        in_specs=[vmem, smem, vmem, vmem, vmem, vmem, vmem],
+        in_specs=[vmem, smem, smem, *[vmem] * 7],
         out_specs=(vmem, vmem),
-        scratch_shapes=[pltpu.VMEM((width, lanes), jnp.float32), pltpu.VMEM((8, lanes), jnp.float32)],
-        compiler_params=pltpu.CompilerParams(vmem_limit_bytes=20 * 1024 * 1024),
-    )(places, order, q_all, kv_all, acc, total, top)
+        scratch_shapes=[
+            pltpu.VMEM((far, width), jnp.bfloat16),
+            pltpu.VMEM((far, width), jnp.bfloat16),
+            pltpu.VMEM((far // width, width, width), jnp.bfloat16),
+            [pltpu.VMEM((marks.shape[0], lanes), jnp.bfloat16)] * 2,
+            pltpu.VMEM(acc.shape, jnp.float32),
+            pltpu.VMEM(total.shape, jnp.float32),
+            pltpu.VMEM((width, lanes), jnp.float32),
+            pltpu.VMEM((8, lanes), jnp.float32),
+        ],
+        compiler_params=pltpu.CompilerParams(vmem_limit_bytes=28 * 1024 * 1024),
+    )(places, order, rank, q_all, kv_all, acc, total, top, q_turned, marks)
 
 
 def return_kernel(o_ref, lse_ref, o_all, lse_all, relay, o_send, o_recv, l_send, l_recv,
@@ -469,8 +534,11 @@
     kv = kv.reshape(2, EACH, 2, span // 2, 2, width).transpose(4, 2, 0, 1, 3, 5)
     kv = kv.reshape(4, 2, EACH, span // 2, width)
     places = span_order.astype(jnp.float32).reshape(RING // 2, 2, ROW, 2, EACH).transpose(0, 3, 1, 2, 4)
+    flat = places.reshape(-1)
     places = jnp.broadcast_to(places.reshape(RING, 2 * ROW * EACH, 1), (RING, 2 * ROW * EACH, 2 * span))
-    o, lse = finish(places, span_order, *attend(places, q, kv))
+    away = (jnp.arange(flat.shape[0]) // (2 * ROW * EACH) - place()[1] + RING + NEAR // 2) % RING >= NEAR
+    rank = jnp.sum((away[None, :] & (flat[None, :] < flat[:, None])).astype(jnp.int32), axis=1)
+    o, lse = finish(places, span_order, rank, *attend(places, q, kv))
 
     o, lse = send_back(o.reshape(ROW, 2, EACH, 2 * span, width), lse.reshape(ROW, 2, EACH, 1, 2 * span))
     o = o.reshape(2, 2, 2, EACH, 2, span, width)

time: 89.2 us -> 79.3 us (0.89)
  Pallas kernels: 82.8 us -> 71.7 us
    pallas_call x1, Pallas kernels: 65.8 us -> 39.7 us  [attend(): pl.pallas_call(attend_kernel, out_shape=(jax.ShapeDtypeStruct((ROW, 2, *q...]
    pallas_call x1, Pallas kernels: 1.02 us -> 15.9 us  [finish(): pl.pallas_call(finish_kernel, out_shape=(jax.ShapeDtypeStruct((tiles, lan...]
where the time goes in v5:
time: 79.3 us; the launch traced here: 78.2 us
  Pallas kernels  71.7 us (90%)
  local copies, waits for them, and re-layouts  4.67 us (6%)
  other arithmetic  1.75 us (2%)
    pallas_call x1, Pallas kernels, attend(): pl.pallas_call(attend_kernel, out_shape=(jax.ShapeDtypeStruct((ROW, 2, *q...  39.7 us
    pallas_call x1, Pallas kernels, send_back(): pl.pallas_call(return_kernel, out_shape=(jax.ShapeDtypeStruct(o.shape, o....  16 us
    pallas_call x1, Pallas kernels, finish(): pl.pallas_call(finish_kernel, out_shape=(jax.ShapeDtypeStruct((tiles, lan...  15.9 us
    another operation x2, local copies, waits for them, and re-layouts, body(): kv = jnp.stack([stored_key_rows, stored_value_rows])  1.85 us

profile of v5, /device:TPU:1, one launch (start us, length us, event | category | flops | bytes accessed | tf_op | source)
XLA Modules:
  0.0 78.2 jit_solution(1866448095485863771)
XLA Ops:
  0.0 0.7 convert_element_type.19
  0.7 0.2 reshape.77
  0.9 0.1 lt.29
  1.0 0.1 broadcast_in_dim.4
  1.1 0.2 convert_reduce_fusion.rank
  1.3 0.1 broadcast_in_dim.5.place_ref
  1.4 0.9 %copy.30 = bf16[1,2,2,64,2,128]{5,3,1,0,2,4:T(8,128)(2,1)S(1)} copy(bf16[1,2,2,64,2,128]{5,4,3,2,1,0:T(2,128)(2,1)} %bitcast.30) | data formatting | bytes 262144 | tf_op jit(solution)/shard_map/stack | solution.py:533
  2.3 0.9 %copy.31 = bf16[1,2,2,64,2,128]{5,3,1,0,2,4:T(8,128)(2,1)S(1)} copy(bf16[1,2,2,64,2,128]{5,4,3,2,1,0:T(2,128)(2,1)} %bitcast.31) | data formatting | bytes 262144 | tf_op jit(solution)/shard_map/stack | solution.py:533
  3.3 1.1 %copy.29 = bf16[2,128,2,2,2,128]{5,1,4,0,3,2:T(8,128)(2,1)S(1)} copy(bf16[2,128,2,2,2,128]{5,4,3,2,1,0:T(2,128)(2,1)} %bitcast.29) | data formatting | bytes 1048576 | tf_op jit(solution)/shard_map/reshape | solution.py:531
  4.4 0.0 copy-start
  4.4 39.7 %shard_map.46 = (bf16[4,2,2,256,128]{4,3,2,1,0:T(8,128)(2,1)S(1)}, bf16[2,8,4,2,2,64,128]{6,5,4,3,2,1,0:T(8,128)(2,1)S(1)}, f32[16,128,256]{2,1,0:T(8,128)S(1)},...) custom-call(f32[8,16,256]{2,1,0:T(8,128)S(1)} %broadcast_in_dim.5.pl, ...), custom_call_target="tpu_custom_call" | custom-call | flops 10000000000 | bytes 20000000 | tf_op jit(solution)/shard_map/pallas_call | solution.py:295
  44.1 0.0 copy-done
  44.2 15.9 %shard_map.47 = (bf16[16,256,128]{2,1,0:T(8,128)(2,1)S(1)}, f32[16,1,256]{2,1,0:T(1,128)S(1)}) custom-call(f32[8,16,256]{2,1,0:T(8,128)S(1)} %broadcast_in_dim.5.place_ref, s32[128]{0:T(128)S(1)} %copy-done, s32[128]{0:T(128)S(1)} %convert_reduce_fusion.rank, bf16[4,2,2,256,128]{4,3,2,1,0:T(8,128)(2,1)S(1)} %get-tuple-element.16.q_all, ...), custom_call_target="tpu_custom_call" | custom-call | tf_op jit(solution)/shard_map/pallas_call | solution.py:457
  60.1 16.0 %shard_map.48 = (bf16[4,2,2,256,128]{4,3,2,1,0:T(8,128)(2,1)S(1)}, f32[4,2,2,1,256]{4,3,2,1,0:T(1,128)S(1)}) custom-call(bf16[4,2,2,256,128]{4,3,2,1,0:T(8,128)(2,1)S(1)} %bitcast.20, f32[4,2,2,1,256]{4,3,2,1,0:T(1,128)S(1)} %bitcast.26), custom_call_target="tpu_custom_call" | custom-call | bytes 20000000 | tf_op jit(solution)/shard_map/pallas_call | solution.py:514
  76.2 0.8 %fusion = bf16[2,2,2,2,128,128]{5,4,3,2,1,0:T(8,128)(2,1)S(1)} fusion(bf16[2,2,2,2,2,128,128]{6,5,4,3,2,1,0:T(8,128)(2,1)S(1)} %bitcast.19, f32[2,2,2,2,2,128]{5,4,3,2,1,0:T(2,128)S(1)} %broadcast_divide_fusion), kind=kLoop, calls=%fused_computation.1 | loop fusion | flops 1310720 | bytes 1589248 | tf_op jit(solution)/shard_map/reduce_sum | solution.py:549
  77.1 1.1 %copy.33 = bf16[256,8,128]{2,1,0:T(8,128)(2,1)} copy(bf16[256,8,128]{2,0,1:T(8,128)(2,1)S(1)} %bitcast.28) | data formatting | bytes 1048576 | tf_op jit(solution)/shard_map/reshape | solution.py:550
  (7 shorter events, 0.2 us)
Async XLA Ops:
  4.4 39.7 %copy-start = (s32[128]{0:T(128)S(1)}, s32[128]{0:T(128)}, u32[]{:S(2)}) copy-start(s32[128]{0:T(128)} %order.1) | copy-start | bytes 1540

commit v6 on v5

--- a/solution.py
+++ b/solution.py
@@ -10,7 +10,7 @@
 ROW = 4
 RING = 8
 EACH = 2
-NEAR = 3
+NEAR = 2
 MESH = pl.DeviceIdType.MESH
 NEVER = 2.0**20
 
@@ -22,6 +22,10 @@
 
 def device(x, z, c, y):
     return (z // 2 * 2 + c, x * 2 + z % 2, y)
+
+
+def row_at(z, n):
+    return (z + jnp.where(n % 2 == 1, -((n + 1) // 2), n // 2) + RING) % RING
 
 
 def greet(peers):
@@ -164,10 +168,6 @@
                 dc = (core + c) % 2
                 arrived(q_all.at[(x + ROW - dx) % ROW, core], q_recv.at[steps.index((dx, 0)) + dc])
 
-    def row_at(n):
-        off = jnp.where(n % 2 == 1, -((n + 1) // 2), n // 2)
-        return off, (z + off + RING) % RING
-
     def weigh(t, zc, buf):
         own = (t // EACH % 2 * ROW + t // (2 * EACH)) * EACH + t % EACH
         before = place_ref[zc] < place_ref[z, pl.ds(own, 1), :]
@@ -209,11 +209,12 @@
 
     per_turn = 2 * EACH
     turns = ROW * NEAR
+    within = min(turns - 1 - NEAR, 2 * ROW)
 
     def plan(m):
         g = m // NEAR
         chip = (x + jnp.where(g == 1, 3, jnp.where(g == 2, 1, jnp.where(g == 3, 2, 0)))) % ROW
-        return chip, chip * per_turn, row_at(m % NEAR)[1]
+        return chip, chip * per_turn, row_at(z, m % NEAR)
 
     def turn(m, carry):
         _, base, zc = plan(m)
@@ -223,7 +224,7 @@
         def _():
             ready(next_zc)
 
-        @pl.when((m >= NEAR) & (m < NEAR + 2 * ROW))
+        @pl.when((m >= NEAR) & (m < NEAR + within))
         def _():
             event = m - NEAR
             t, j = event // ROW + 2, event % ROW
@@ -253,17 +254,22 @@
 
     weigh(x * per_turn, z, 0)
     lax.fori_loop(0, turns - 1, turn, 0)
-    for up_j, down_j in ((0, 3), (1, 2)):
-        rise(RING // 2, up_j)
-        fall(RING // 2, down_j)
     _, last_base, last_zc = plan(turns - 1)
     for u in range(per_turn):
         if u < per_turn - 1:
             weigh(last_base + u + 1, last_zc, 1 - u % 2)
         absorb(last_base + u, last_zc, u % 2)
-    for r in range(2, RING - 1):
-        for j in range(ROW):
-            arrived(kv_all.at[1 - c, (z + r) % RING, (x + j) % ROW], core_recv.at[r, j])
+    for event in range(within, 2 * ROW):
+        for hop in (rise, fall):
+            hop(event // ROW + 2, (0, 1, 3, 2)[event % ROW])
+    for up_j, down_j in ((0, 3), (1, 2)):
+        rise(RING // 2, up_j)
+        fall(RING // 2, down_j)
+    near = [(RING - (n + 1) // 2 if n % 2 else n // 2) % RING for n in range(NEAR)]
+    for r in range(RING):
+        if r not in near:
+            for j in range(ROW):
+                arrived(kv_all.at[1 - c, (z + r) % RING, (x + j) % ROW], core_recv.at[r, j])
 
     for j in range(ROW):
         for t in range(RING // 2):
@@ -342,8 +348,7 @@
 
     def sort(i, carry):
         n, g = i // (2 * ROW), i % (2 * ROW)
-        off = jnp.where(n % 2 == 1, (n + 3) // 2, -((n + 4) // 2))
-        zc = (z + off + RING) % RING
+        zc = row_at(z, n + NEAR)
         core, at_x = g // ROW, g % ROW
         for b in range(EACH):
             at = pl.multiple_of(rank[((zc * 2 + core) * ROW + at_x) * EACH + b] * piece, piece)
@@ -533,7 +538,7 @@
     kv = jnp.stack([stored_key_rows, stored_value_rows])
     kv = kv.reshape(2, EACH, 2, span // 2, 2, width).transpose(4, 2, 0, 1, 3, 5)
     kv = kv.reshape(4, 2, EACH, span // 2, width)
-    places = span_order.astype(jnp.float32).reshape(RING // 2, 2, ROW, 2, EACH).transpose(0, 3, 1, 2, 4)
+    places = span_order.reshape(RING // 2, 2, ROW, 2, EACH).transpose(0, 3, 1, 2, 4)
     flat = places.reshape(-1)
     places = jnp.broadcast_to(places.reshape(RING, 2 * ROW * EACH, 1), (RING, 2 * ROW * EACH, 2 * span))
     away = (jnp.arange(flat.shape[0]) // (2 * ROW * EACH) - place()[1] + RING + NEAR // 2) % RING >= NEAR

time: 79.3 us -> 84.4 us (1.064)
  the two profiles are of different devices: /device:TPU:1 before, /device:TPU:121 now
where the time goes in v6:
time: 84.4 us; the launch traced here: 83.1 us
  Pallas kernels  76.6 us (91%)
  local copies, waits for them, and re-layouts  5.32 us (6%)
  other arithmetic  1.1 us (1%)
    pallas_call x1, Pallas kernels, attend(): pl.pallas_call(attend_kernel, out_shape=(jax.ShapeDtypeStruct((ROW, 2, *q...  38.1 us
    pallas_call x1, Pallas kernels, finish(): pl.pallas_call(finish_kernel, out_shape=(jax.ShapeDtypeStruct((tiles, lan...  22.8 us
    pallas_call x1, Pallas kernels, send_back(): pl.pallas_call(return_kernel, out_shape=(jax.ShapeDtypeStruct(o.shape, o....  15.7 us
    another operation x2, local copies, waits for them, and re-layouts, body(): kv = jnp.stack([stored_key_rows, stored_value_rows])  1.85 us

profile of v6, /device:TPU:121, one launch (start us, length us, event | category | flops | bytes accessed | tf_op | source)
XLA Modules:
  0.0 83.1 jit_solution(14090996216764043437)
XLA Ops:
  0.0 0.8 reshape.77
  0.9 0.1 lt.29
  1.0 0.1 broadcast_in_dim.4
  1.1 0.2 convert_reduce_fusion.rank
  1.3 0.1 broadcast_in_dim.5.place_ref
  1.4 0.9 %copy.30 = bf16[1,2,2,64,2,128]{5,3,1,0,2,4:T(8,128)(2,1)S(1)} copy(bf16[1,2,2,64,2,128]{5,4,3,2,1,0:T(2,128)(2,1)} %bitcast.30) | data formatting | bytes 262144 | tf_op jit(solution)/shard_map/stack | solution.py:538
  2.3 0.9 %copy.31 = bf16[1,2,2,64,2,128]{5,3,1,0,2,4:T(8,128)(2,1)S(1)} copy(bf16[1,2,2,64,2,128]{5,4,3,2,1,0:T(2,128)(2,1)} %bitcast.31) | data formatting | bytes 262144 | tf_op jit(solution)/shard_map/stack | solution.py:538
  3.3 1.1 %copy.29 = bf16[2,128,2,2,2,128]{5,1,4,0,3,2:T(8,128)(2,1)S(1)} copy(bf16[2,128,2,2,2,128]{5,4,3,2,1,0:T(2,128)(2,1)} %bitcast.29) | data formatting | bytes 1048576 | tf_op jit(solution)/shard_map/reshape | solution.py:536
  4.4 0.0 copy-start
  4.4 38.1 %shard_map.46 = (bf16[4,2,2,256,128]{4,3,2,1,0:T(8,128)(2,1)S(1)}, bf16[2,8,4,2,2,64,128]{6,5,4,3,2,1,0:T(8,128)(2,1)S(1)}, f32[16,128,256]{2,1,0:T(8,128)S(1)},...) custom-call(s32[8,16,256]{2,1,0:T(8,128)S(1)} %broadcast_in_dim.5.pl, ...), custom_call_target="tpu_custom_call" | custom-call | flops 10000000000 | bytes 20000000 | tf_op jit(solution)/shard_map/pallas_call | solution.py:301
  42.5 0.0 copy-done
  42.5 22.8 %shard_map.47 = (bf16[16,256,128]{2,1,0:T(8,128)(2,1)S(1)}, f32[16,1,256]{2,1,0:T(1,128)S(1)}) custom-call(s32[8,16,256]{2,1,0:T(8,128)S(1)} %broadcast_in_dim.5.place_ref, s32[128]{0:T(128)S(1)} %copy-done, s32[128]{0:T(128)S(1)} %convert_reduce_fusion.rank, bf16[4,2,2,256,128]{4,3,2,1,0:T(8,128)(2,1)S(1)} %get-tuple-element.16.q_all, ...), custom_call_target="tpu_custom_call" | custom-call | tf_op jit(solution)/shard_map/pallas_call | solution.py:462
  65.3 15.7 %shard_map.48 = (bf16[4,2,2,256,128]{4,3,2,1,0:T(8,128)(2,1)S(1)}, f32[4,2,2,1,256]{4,3,2,1,0:T(1,128)S(1)}) custom-call(bf16[4,2,2,256,128]{4,3,2,1,0:T(8,128)(2,1)S(1)} %bitcast.20, f32[4,2,2,1,256]{4,3,2,1,0:T(1,128)S(1)} %bitcast.26), custom_call_target="tpu_custom_call" | custom-call | bytes 20000000 | tf_op jit(solution)/shard_map/pallas_call | solution.py:519
  81.1 0.8 fusion
  82.0 1.1 %copy.33 = bf16[256,8,128]{2,1,0:T(8,128)(2,1)} copy(bf16[256,8,128]{2,0,1:T(8,128)(2,1)S(1)} %bitcast.28) | data formatting | bytes 1048576 | tf_op jit(solution)/shard_map/reshape | solution.py:555
  (7 shorter events, 0.2 us)
Async XLA Ops:
  4.4 38.1 %copy-start = (s32[128]{0:T(128)S(1)}, s32[128]{0:T(128)}, u32[]{:S(2)}) copy-start(s32[128]{0:T(128)} %order.1) | copy-start | bytes 1540
